TPU v7x, 256 devices: a whole 4x4x8 slice. The times are simulated.
256 devices in a mesh: rows: 64 (over z, x, core), grp: 4 (over y).
Axes of the slice: x: 4, y: 4, z: 8, core: 2. Of those that a mesh axis runs over, the one named last changes fastest.
Arguments:
- user_features: bfloat16 [4, 16384, 256], P('grp', 'rows'), may hold values from -72 to 72
- w_first: bfloat16 [256, 256], replicated, may hold values from -0.375 to 0.375
- w_second: bfloat16 [256, 256], replicated, may hold values from -0.375 to 0.375
- item_embed: bfloat16 [4, 16384, 256], P('grp', 'rows'), may hold values from -27 to 27
- example_weight: float32 [4, 16384], P('grp', 'rows'), may hold values from 0.02 to 0.2
- positive: int32 [4, 16384], P('grp', 'rows'), may hold values from 0 to 16383
- item_owner: int32 [4, 16384, 1], P('grp', 'rows'), may hold values from 0 to 63; in each aligned block of 256 rows (0 to 255, 256 to 511, ..., all dimensions but the last counted through in order) at most 16 rows name the same one
- item_row: int32 [4, 16384], P('grp', 'rows'), may hold values from 0 to 4095
Outputs:
- grad_first: float32 [256, 256], replicated
- grad_second: float32 [256, 256], replicated
- grad_table: float32 [262144, 256], P('rows', 'grp')
Inputs may be any that keep to these rules, and one draw needn't show every extreme that they name: `item_owner`: within the rows of one device (aligned blocks of 256 pairs of a group) no owner is named by more than 16 pairs, a bound that some block reaches.
All inputs are finite; a program needn't handle non-finite values.
Results may differ from a plain program's by a relative error of at most 0.0023.
The roundings to bfloat16 on the way count: a program that leaves them out, or rounds other values in their place, can miss the bound.
Values may be sent and summed in bfloat16 or wider, within the bound.
A program may use at most 128 MiB of HBM per device.

v0:
```python
import jax
import jax.numpy as jnp
from jax import lax
from jax.sharding import Mesh
from jax.sharding import PartitionSpec as P

ITEMS_DEV = 4096
ROWS = ("rows_0", "rows_1", "rows_2")
ROWS_GRP = ("rows_0", "rows_1", "rows_2", "grp")


def gather_turned(arrays, axis, dims):
    turned = [jnp.moveaxis(a, dim, 0) for a, dim in zip(arrays, dims)]
    widths = [t[0].size for t in turned]
    both = jnp.concatenate([t.reshape(-1, w) for t, w in zip(turned, widths)], axis=1)
    filled = lax.all_gather(both, axis, axis=0, tiled=True)
    tiles = jnp.split(filled, [sum(widths[:k]) for k in range(1, len(widths))], axis=1)
    return tuple(
        (
            jnp.moveaxis(b.reshape(-1, *t.shape[1:]), 0, dim)
            for b, t, dim in zip(tiles, turned, dims)
        )
    )


def cut_along(value, dim, count):
    before, after = (value.shape[:dim], value.shape[dim + 1 :])
    return jnp.moveaxis(value.reshape(*before, count, -1, *after), dim, 0)


def sum_at_owner(value, axis, dim):
    count = lax.axis_size(axis)
    tiles = lax.all_to_all(cut_along(value, dim, count), axis, 0, 0, tiled=True)
    return jnp.sum(tiles, axis=0)


def summed_rows(value, axes, dim):
    far, near = axes
    tiles = cut_along(value, dim, lax.axis_size(far))
    nearer = sum_at_owner(tiles, near, dim + 1)
    arrived = lax.all_to_all(nearer, far, split_axis=0, concat_axis=0, tiled=True)
    return arrived.sum(axis=0)


def padded_to(lines, count):
    spare = -lines.shape[0] % count
    if not spare:
        return lines
    return jnp.concatenate([lines, jnp.zeros((spare, *lines.shape[1:]), lines.dtype)])


def sent_to_all(value, axis):
    count = lax.axis_size(axis)
    return lax.all_to_all(
        jnp.broadcast_to(value[None], (count, *value.shape)), axis, 0, 0, tiled=True
    )


def joined_along(tiles, dim):
    shape = list(tiles.shape[1:])
    shape[dim] *= tiles.shape[0]
    return jnp.moveaxis(tiles, 0, dim).reshape(shape)


def gather_axes(value, axes, dim):
    far, near = axes
    tiles = sent_to_all(sent_to_all(value, far), near)
    return joined_along(tiles.swapaxes(0, 1).reshape(-1, *value.shape), dim)


def total_of(value, axes):
    own = summed_rows(padded_to(value, lax.axis_size(axes[0]) * lax.axis_size(axes[1])), axes, 0)
    whole = gather_axes(own, axes, 0)
    return whole[: len(value)].reshape(value.shape)


def in_one(arrays, axis):
    flat, at, done = (jnp.concatenate([a.reshape(-1) for a in arrays]), 0, [])
    total = total_of(flat, axis)
    for a in arrays:
        done.append(total[at : at + a.size].reshape(a.shape))
        at += a.size
    return tuple(done)


def one_exchange(value, axis, axes, splits, concats):
    sizes = [lax.axis_size(a) for a in axes]
    tiles = cut_along(value, splits[0], sizes[0])
    tiles = jnp.moveaxis(cut_along(tiles, splits[1] + 1, sizes[1]), 0, 1)
    inside = tiles.shape[2:]
    tiles = tiles.reshape(-1, *inside)
    tiles = lax.all_to_all(tiles, axis, split_axis=0, concat_axis=0, tiled=True)
    tiles = joined_along(tiles.reshape(*sizes, *inside), concats[0] + 1)
    return joined_along(tiles, concats[1])


def contract_first(left, right):
    return lax.dot_general(
        left, right, (((0,), (0,)), ((), ())), preferred_element_type=jnp.float32
    )


def contract_last(left, right):
    return lax.dot_general(
        left, right, (((1,), (1,)), ((), ())), preferred_element_type=jnp.float32
    )


def body(
    user_features, w_first, w_second, item_embed, example_weight, positive, item_owner, item_row
):
    features = user_features[0]
    own_items = item_embed[0]
    weights = example_weight[0]
    targets = positive[0]
    owners = item_owner[0, :, 0]
    item_rows = item_row[0]
    my_users = features.shape[0]
    feature_width = own_items.shape[1]
    peers = lax.axis_size(ROWS)
    my_index = lax.axis_index(ROWS)
    pre_act = jnp.dot(features, w_first, preferred_element_type=jnp.float32)
    hidden = jax.nn.silu(pre_act).astype(jnp.bfloat16)
    user_vecs = jnp.dot(hidden, w_second, preferred_element_type=jnp.float32).astype(jnp.bfloat16)
    gathered = lax.all_gather(own_items, ROWS, axis=0, tiled=True)
    group_users = gathered.shape[0]
    scores = contract_last(user_vecs, gathered)
    row_max = jnp.max(scores, axis=1, keepdims=True)
    log_total = row_max + jnp.log(jnp.sum(jnp.exp(scores - row_max), axis=1, keepdims=True))
    columns = lax.broadcasted_iota(jnp.int32, (1, group_users), 1)
    chosen = (columns == targets[:, None]).astype(jnp.float32)
    dscore = (weights[:, None] * (jnp.exp(scores - log_total) - chosen)).astype(jnp.bfloat16)
    grad_user = jnp.dot(dscore, gathered, preferred_element_type=jnp.float32).astype(jnp.bfloat16)
    everyone = lax.all_gather(user_vecs, ROWS, axis=0, tiled=True)
    target_all, total_all, weight_all = gather_turned(
        (targets.astype(jnp.float32), log_total[:, 0], weights), ROWS, (0, 0, 0)
    )
    back_scores = contract_last(everyone, own_items)
    own_columns = my_index * my_users + lax.broadcasted_iota(jnp.int32, (1, my_users), 1)
    hits = (own_columns == target_all.astype(jnp.int32)[:, None]).astype(jnp.float32)
    back_dscore = (weight_all[:, None] * (jnp.exp(back_scores - total_all[:, None]) - hits)).astype(
        jnp.bfloat16
    )
    grad_item = contract_first(back_dscore, everyone)
    d_second = contract_first(hidden, grad_user)
    back_grad = contract_last(grad_user, w_second)
    sigmoid_pre = jax.nn.sigmoid(pre_act)
    grad_pre = (back_grad * sigmoid_pre * (1.0 + pre_act * (1.0 - sigmoid_pre))).astype(
        jnp.bfloat16
    )
    d_first = contract_first(features, grad_pre)
    grad_first, grad_second = in_one((d_first, d_second), (("rows_0", "rows_1"), ("rows_2", "grp")))
    capacity = max(2, 4 * my_users // peers)
    member = (owners[:, None] == lax.broadcasted_iota(jnp.int32, (1, peers), 1)).astype(jnp.int32)
    before = jnp.cumsum(member, axis=0) - member
    slot_rank = jnp.sum(before * member, axis=1)
    slots = owners * capacity + slot_rank
    send_grad = jnp.zeros((peers * capacity, feature_width), jnp.float32).at[slots].set(grad_item)
    send_grad = send_grad.reshape(peers, capacity, feature_width)
    send_rows = (
        jnp.full((peers * capacity,), -1.0, jnp.float32)
        .at[slots]
        .set(item_rows.astype(jnp.float32))
    )
    groups = lax.axis_size("grp")
    rows_wide = jnp.broadcast_to(send_rows.reshape(peers, capacity, 1), (peers, capacity, groups))
    got_grad, got_rows = (
        one_exchange(send_grad, ROWS_GRP, (ROWS, "grp"), (0, 2), (0, 1)),
        one_exchange(rows_wide, ROWS_GRP, (ROWS, "grp"), (0, 2), (0, 1)),
    )
    share_width = feature_width // groups
    table_rows = got_rows.reshape(-1).astype(jnp.int32)
    table_rows = jnp.where(table_rows >= 0, table_rows, ITEMS_DEV)
    grad_table = (
        jnp.zeros((ITEMS_DEV, share_width), jnp.float32)
        .at[table_rows]
        .add(got_grad.reshape(-1, share_width), mode="drop")
    )
    return (grad_first, grad_second, grad_table)


def solution(mesh):
    torus = Mesh(
        mesh.devices.reshape(8, 4, 2, mesh.shape["grp"]), ("rows_0", "rows_1", "rows_2", "grp")
    )
    placed = (
        P("grp", ROWS, None),
        P(),
        P(),
        P("grp", ROWS, None),
        P("grp", ROWS),
        P("grp", ROWS),
        P("grp", ROWS, None),
        P("grp", ROWS),
    )
    return jax.shard_map(
        body, mesh=torus, in_specs=placed, out_specs=(P(), P(), P(ROWS, "grp")), check_vma=False
    )
```

profile of v0, /device:TPU:1, one launch (start us, length us, event | category | flops | bytes accessed | tf_op | source)
XLA Modules:
  0.0 337.8 jit_solution(12011691266853101209)
XLA Ops:
  13.0 84.9 %all-gather.6.cloned.1.call-done = bf16[1,16384,256]{2,1,0:T(8,128)(2,1)} async-done(((bf16[1,256,256]{2,1,0:T(8,128)(2,1)}), bf16[1,16384,256]{2,1,0:T(8,128)(2,1)}) %all-gather.6.cloned.1.call-update) | async-done | bytes 8388624 | tf_op jit(solution)/shard_map/all_gather | solution.py:125
  97.9 11.6 %fusion.36 = (f32[256]{0:T(256)S(1)}, f32[256,16384]{1,0:T(8,128)}) fusion(bf16[256,256]{1,0:T(8,128)(2,1)} %convolution_convert_fusion, bf16[1,16384,256]{2,1,0:T(8,128)(2,1)} %all-gather.6.cloned.1.call-done), kind=kOutput, calls=%fused_computation.61 | convolution fusion | flops 2151677696 | bytes 25297920 | tf_op jit(solution)/shard_map/dot_general | solution.py:104
  109.5 8.3 %exponential_reduce_fusion = f32[256]{0:T(256)S(1)} fusion(f32[256,16384]{1,0:T(8,128)} %get-tuple-element.21, f32[256]{0:T(256)S(1)} %get-tuple-element.20), kind=kLoop, calls=%fused_computation.10 | loop fusion | flops 8388352 | bytes 16779264 | tf_op jit(solution)/shard_map/reduce_sum | solution.py:129
  117.8 13.0 %fusion.11 = bf16[256,256]{1,0:T(8,128)(2,1)S(1)} fusion(bf16[1,16384,256]{2,1,0:T(8,128)(2,1)} %all-gather.6.cloned.1.call-done, f32[256,16384]{1,0:T(8,128)} %get-tuple-element.21, s32[256]{0:T(256)S(1)} %bitcast.120, f32[256]{0:T(256)S(1)} %log_add_fusion, f32[256]{0:T(256)S(1)} %bitcast.116), kind=kOutput, calls=%fused_computation.21 | convolution fusion | flops 2172715008 | bytes 25299968 | tf_op jit(solution)/shard_map/dot_general | solution.py:133
  133.1 4.5 %all-to-all-start = ((f32[8,32,512]{2,1,0:T(8,128)}), f32[8,32,512]{2,1,0:T(8,128)S(1)}, u32[]{:S(2)}, u32[]{:S(2)}) async-start(f32[8,32,512]{2,1,0:T(8,128)} %copy.25), calls=%async_computation | async-start | bytes 1048576 | tf_op jit(solution)/shard_map/all_to_all | solution.py:33
  137.6 1.4 scatter_custom_fusion
  139.1 7.8 %all-to-all-done = f32[8,32,512]{2,1,0:T(8,128)S(1)} async-done(((f32[8,32,512]{2,1,0:T(8,128)}), f32[8,32,512]{2,1,0:T(8,128)S(1)}, u32[]{:S(2)}, u32[]{:S(2)}) %all-to-all-start) | async-done | bytes 524320 | tf_op jit(solution)/shard_map/all_to_all | solution.py:33
  147.7 5.1 %all-to-all-start.1 = ((f32[32,1,512]{2,1,0:T(1,128)}), f32[32,1,512]{2,1,0:T(1,128)S(1)}, u32[]{:S(2)}, u32[]{:S(2)}) async-start(f32[32,1,512]{2,1,0:T(1,128)} %all_to_all.23), calls=%async_computation.1 | async-start | bytes 131072 | tf_op jit(solution)/shard_map/all_to_all | solution.py:41
  152.8 45.7 %all_gather.10 = f32[16384,3]{0,1:T(4,128)S(1)} all-gather(f32[256,3]{0,1:T(4,128)S(1)} %pad_maximum_fusion), channel_id=1, replica_groups=mesh['rows_0'=8,'rows_1'=4,'rows_2'=2,'grp'=4] {'rows_0','rows_1','rows_2'}, dimensions={0}, use_global_device_ids=true | all-gather | bytes 199680 | tf_op jit(solution)/shard_map/all_gather | solution.py:16
  199.2 6.6 %all-to-all-start.2 = ((f32[32,1,512]{2,1,0:T(1,128)}), f32[32,1,512]{2,1,0:T(1,128)S(1)}, u32[]{:S(2)}, u32[]{:S(2)}) async-start(f32[32,1,512]{2,1,0:T(1,128)} %broadcast_in_dim.17), calls=%async_computation.2 | async-start | bytes 131072 | tf_op jit(solution)/shard_map/all_to_all | solution.py:54
  206.0 8.7 %all-to-all-done.2 = f32[32,1,512]{2,1,0:T(1,128)S(1)} async-done(((f32[32,1,512]{2,1,0:T(1,128)}), f32[32,1,512]{2,1,0:T(1,128)S(1)}, u32[]{:S(2)}, u32[]{:S(2)}) %all-to-all-start.2) | async-done | bytes 65568 | tf_op jit(solution)/shard_map/all_to_all | solution.py:54
  215.4 6.6 %all-to-all-start.4 = ((f32[256,1,16,1]{2,3,1,0:T(1,128)}), f32[256,1,16,1]{2,3,1,0:T(1,128)S(1)}, u32[]{:S(2)}, u32[]{:S(2)}) async-start(f32[256,1,16,1]{2,3,1,0:T(1,128)} %bitcast.14), calls=%async_computation.4 | async-start | bytes 262144 | tf_op jit(solution)/shard_map/all_to_all | solution.py:92
  222.0 12.5 %fusion.3.clone.4 = bf16[16384,256]{1,0:T(8,128)(2,1)} fusion(bf16[16384,256]{1,0:T(8,128)(2,1)} %all-gather.4.cloned.1.call-done, s32[256]{0:T(256)S(1)} %iota_add_fusion, f32[16384]{0:T(1024)S(1)} %bitcast.109, f32[16384]{0:T(1024)S(1)} %bitcast.110, s32[16384]{0:T(1024)S(1)} %bitcast.108, bf16[1,256,256]{2,1,0:T(8,128)(2,1)S(1)} %copy-done.1), kind=kOutput, calls=%fused_computation.7.clone.clone.clone.1 | convolution fusion | flops 2172649472 | bytes 17105920 | tf_op jit(solution)/shard_map/dot_general | solution.py:104
  235.7 6.1 %all-to-all-start.3 = ((f32[8,32,512]{2,1,0:T(8,128)}), f32[8,32,512]{2,1,0:T(8,128)}, u32[]{:S(2)}, u32[]{:S(2)}) async-start(f32[8,32,512]{2,1,0:T(8,128)} %broadcast_in_dim.19), calls=%async_computation.3 | async-start | bytes 1048576 | tf_op jit(solution)/shard_map/all_to_all | solution.py:54
  241.8 8.1 %fusion.8 = f32[256,256]{1,0:T(8,128)S(1)} fusion(bf16[16384,256]{1,0:T(8,128)(2,1)} %all-gather.4.cloned.1.call-done, bf16[16384,256]{1,0:T(8,128)(2,1)} %fusion.3.clone.4), kind=kOutput, calls=%fused_computation.15 | convolution fusion | flops 2147483648 | bytes 17039360 | tf_op jit(solution)/shard_map/dot_general | solution.py:98
  249.9 1.7 scatter_custom_fusion.1
  252.5 1.5 copy.29
  254.0 3.4 %reshape.203 = f32[256,1,1024]{2,1,0:T(1,128)} reshape(f32[256,1,16,64]{3,2,1,0:T(8,128)} %bitcast.104) | data formatting | bytes 2097152
  257.5 12.3 %all-to-all-start.5 = ((f32[256,1,1024]{2,1,0:T(1,128)}), f32[256,1,1024]{2,1,0:T(1,128)S(1)}, u32[]{:S(2)}, u32[]{:S(2)}) async-start(f32[256,1,1024]{2,1,0:T(1,128)} %reshape.203), calls=%async_computation.5 | async-start | bytes 2097152 | tf_op jit(solution)/shard_map/all_to_all | solution.py:92
  273.0 27.7 %all-to-all-done.5 = f32[256,1,1024]{2,1,0:T(1,128)S(1)} async-done(((f32[256,1,1024]{2,1,0:T(1,128)}), f32[256,1,1024]{2,1,0:T(1,128)S(1)}, u32[]{:S(2)}, u32[]{:S(2)}) %all-to-all-start.5) | async-done | bytes 1048608 | tf_op jit(solution)/shard_map/all_to_all | solution.py:92
  301.2 3.1 reduce.3
  304.3 1.9 reshape.204
  306.2 23.2 %scatter_custom_fusion.2 = f32[4096,64]{1,0:T(8,128)S(1)} fusion(s32[4096]{0:T(1024)S(1)} %bitcast.111, f32[4096,64]{1,0:T(8,128)} %bitcast.105, f32[]{:T(128)} %constant.18.clone.1), kind=kCustom, calls=%fused_computation.22 | custom fusion | flops 262144 | bytes 1049088 | tf_op jit(solution)/shard_map/scatter-add | solution.py:177
  329.4 1.6 copy.31
  (60 shorter events, 16.1 us)
Async XLA Ops:
  7.2 2.0 copy-start
  7.2 90.7 %all-gather.6.cloned.1.call-start = ((), (), s32[]{:S(2)}) async-start(), calls=%async_computation.7 | async-start | bytes 8519680 | tf_op jit(solution)/shard_map/all_gather | solution.py:125
  7.9 214.1 %all-gather.4.cloned.1.call-start = ((), (), s32[]{:S(2)}) async-start(), calls=%async_computation.6 | async-start | bytes 8519680 | tf_op jit(solution)/shard_map/all_gather | solution.py:134
  109.5 8.3 %copy-start.4 = (f32[1,256]{1,0:T(1,128)S(1)}, f32[1,256]{1,0:T(1,128)}, u32[]{:S(2)}) copy-start(f32[1,256]{1,0:T(1,128)} %param.12) | copy-start | bytes 3076
  109.5 8.3 %copy-start.5 = (s32[1,256]{1,0:T(1,128)S(1)}, s32[1,256]{1,0:T(1,128)}, u32[]{:S(2)}) copy-start(s32[1,256]{1,0:T(1,128)} %param.13) | copy-start | bytes 3076
  117.8 13.4 %copy-start.2 = (bf16[1,256,256]{2,1,0:T(8,128)(2,1)S(1)}, bf16[1,256,256]{2,1,0:T(8,128)(2,1)}, u32[]{:S(2)}) copy-start(bf16[1,256,256]{2,1,0:T(8,128)(2,1)} %param.8) | copy-start | bytes 393220
  117.8 19.8 %copy-start.3 = (s32[1,256,1]{1,2,0:T(1,128)S(1)}, s32[1,256,1]{1,2,0:T(1,128)}, u32[]{:S(2)}) copy-start(s32[1,256,1]{1,2,0:T(1,128)} %param.14) | copy-start | bytes 3076
  130.9 91.1 %copy-start.1 = (bf16[1,256,256]{2,1,0:T(8,128)(2,1)S(1)}, bf16[1,256,256]{2,1,0:T(8,128)(2,1)}, u32[]{:S(2)}) copy-start(bf16[1,256,256]{2,1,0:T(8,128)(2,1)} %param.11) | copy-start | bytes 393220
  133.1 13.9 %all-to-all-start = ((f32[8,32,512]{2,1,0:T(8,128)}), f32[8,32,512]{2,1,0:T(8,128)S(1)}, u32[]{:S(2)}, u32[]{:S(2)}) async-start(f32[8,32,512]{2,1,0:T(8,128)} %copy.25), calls=%async_computation | async-start | bytes 1048576 | tf_op jit(solution)/shard_map/all_to_all | solution.py:33
  147.7 50.8 %all-to-all-start.1 = ((f32[32,1,512]{2,1,0:T(1,128)}), f32[32,1,512]{2,1,0:T(1,128)S(1)}, u32[]{:S(2)}, u32[]{:S(2)}) async-start(f32[32,1,512]{2,1,0:T(1,128)} %all_to_all.23), calls=%async_computation.1 | async-start | bytes 131072 | tf_op jit(solution)/shard_map/all_to_all | solution.py:41
  199.2 15.5 %all-to-all-start.2 = ((f32[32,1,512]{2,1,0:T(1,128)}), f32[32,1,512]{2,1,0:T(1,128)S(1)}, u32[]{:S(2)}, u32[]{:S(2)}) async-start(f32[32,1,512]{2,1,0:T(1,128)} %broadcast_in_dim.17), calls=%async_computation.2 | async-start | bytes 131072 | tf_op jit(solution)/shard_map/all_to_all | solution.py:54
  215.4 19.4 %all-to-all-start.4 = ((f32[256,1,16,1]{2,3,1,0:T(1,128)}), f32[256,1,16,1]{2,3,1,0:T(1,128)S(1)}, u32[]{:S(2)}, u32[]{:S(2)}) async-start(f32[256,1,16,1]{2,3,1,0:T(1,128)} %bitcast.14), calls=%async_computation.4 | async-start | bytes 262144 | tf_op jit(solution)/shard_map/all_to_all | solution.py:92
  235.7 21.8 %all-to-all-start.3 = ((f32[8,32,512]{2,1,0:T(8,128)}), f32[8,32,512]{2,1,0:T(8,128)}, u32[]{:S(2)}, u32[]{:S(2)}) async-start(f32[8,32,512]{2,1,0:T(8,128)} %broadcast_in_dim.19), calls=%async_computation.3 | async-start | bytes 1048576 | tf_op jit(solution)/shard_map/all_to_all | solution.py:54
  257.5 43.2 %all-to-all-start.5 = ((f32[256,1,1024]{2,1,0:T(1,128)}), f32[256,1,1024]{2,1,0:T(1,128)S(1)}, u32[]{:S(2)}, u32[]{:S(2)}) async-start(f32[256,1,1024]{2,1,0:T(1,128)} %reshape.203), calls=%async_computation.5 | async-start | bytes 2097152 | tf_op jit(solution)/shard_map/all_to_all | solution.py:92
Sparse Core Ops, SparseCore 0:
  10.8 87.1 all-gather.5
  101.3 79.9 all-gather.3
where the time goes:
time: 338 us
  waiting for transfers between devices  130 us (38%)
  matrix products  48 us (14%)
  blocking collectives  45.7 us (14%)
  starting transfers between devices  41.3 us (12%)
  other arithmetic  37.8 us (11%)
  local copies, waits for them, and re-layouts  20.6 us (6%)
  between operations  14.3 us (4%)
    all_gather x1, waiting for transfers between devices, body(): gathered = lax.all_gather(own_items, ROWS, axis=0, tiled=True)  84.9 us
    all_gather x1, blocking collectives, gather_turned(): filled = lax.all_gather(both, axis, axis=0, tiled=True)  45.7 us
    all_to_all x2, waiting for transfers between devices, one_exchange(): tiles = lax.all_to_all(tiles, axis, split_axis=0, concat_axis=0, tiled=True)  27.9 us
    dot_general x2, matrix products, contract_last(): lax.dot_general(left, right, (((1,), (1,)), ((), ())), preferred_element_...  24.1 us
    scatter-add x1, other arithmetic, body(): grad_table = jnp.zeros((ITEMS_DEV, share_width), jnp.float32).at[table_ro...  23.2 us
    all_to_all x2, starting transfers between devices, one_exchange(): tiles = lax.all_to_all(tiles, axis, split_axis=0, concat_axis=0, tiled=True)  18.9 us
    dot_general x1, matrix products, body(): jnp.dot(dscore, gathered, preferred_element_type=jnp.float32)  13 us
    all_to_all x2, starting transfers between devices, sent_to_all(): lax.all_to_all(jnp.broadcast_to(value[None], (count, *value.shape)), axis...  12.7 us
  transfers between devices with their start and end apart: 8, of which 5 were waited for; matrix products, arithmetic and copies ran while one was open for 22% of the time, Pallas kernels for 0%

commit v1 on v0

v1 whole, which is shorter than its diff:
```python
import functools
import jax
import jax.numpy as jnp
from jax import lax
from jax.experimental import pallas as pl
from jax.experimental.pallas import tpu as pltpu
from jax.sharding import Mesh
from jax.sharding import PartitionSpec as P

ITEMS_DEV = 4096
ROWS = ("rows_0", "rows_1", "rows_2")
ROWS_GRP = ("rows_0", "rows_1", "rows_2", "grp")
MESH = pl.DeviceIdType.MESH
F32 = jnp.float32
BF16 = jnp.bfloat16


def chain_length(n, way, half):
    return n // 2 if (way == 0) == (half == 0) else n // 2 - 1


def contract(left, right, dims):
    return lax.dot_general(left, right, ((dims[:1], dims[1:]), ((), ())), preferred_element_type=F32)


def block_kernel(
    nz, nx, nc, feat_ref, w1_ref, w2_ref, items_ref, meta_ref, gi_ref, df_ref,
    users, items_all, items_turned, meta_all, peaks, sums, lses, scale, probs, ds,
    gi_part, gu_part, gu_pair, z_land, x_land, pre_keep, hid_keep,
    z_send, z_recv, x_send, x_recv, p_send, p_recv, m_send, m_recv, l_send, l_recv,
    zr_send, zr_recv, d_send, d_recv, xr_send, xr_recv,
):
    z, x, c = lax.axis_index("rows_0"), lax.axis_index("rows_1"), lax.axis_index("rows_2")
    size = items_ref.shape[0]
    half_size = size // 2
    peers = nx * nc
    me = x * nc + c
    signs = (1, -1)

    def z_at(step):
        return lax.rem(z + step + nz, nz)

    def x_at(step):
        return lax.rem(x + step + nx, nx)

    def peer(step):
        dx, dc = divmod(step, nc)
        return {"rows_1": x_at(dx), "rows_2": lax.rem(c + dc, nc)}

    def from_peer(step):
        dx, dc = divmod(step, nc)
        return x_at(-dx) * nc + lax.rem(c + nc - dc, nc)

    partner = {"rows_2": 1 - c}
    pending = []

    def send(src, dst, send_sem, recv_sem, where):
        copy = pltpu.make_async_remote_copy(
            src_ref=src, dst_ref=dst, send_sem=send_sem, recv_sem=recv_sem,
            device_id=where, device_id_type=MESH,
        )
        copy.start()
        pending.append(copy)

    def arrived(ref, recv_sem):
        pltpu.make_async_copy(ref, ref, recv_sem).wait()

    barrier = pltpu.get_barrier_semaphore()
    for step in range(1, peers):
        pl.semaphore_signal(barrier, inc=1, device_id=peer(step), device_id_type=MESH)
    for sign in signs:
        pl.semaphore_signal(
            barrier, inc=1, device_id={"rows_0": z_at(sign)}, device_id_type=MESH
        )

    def rows_of(block, half):
        return pl.ds(pl.multiple_of(block * size + half * half_size, half_size), half_size)

    def block_rows(block):
        return pl.ds(pl.multiple_of(block * size, size), size)

    pre = jnp.dot(feat_ref[...], w1_ref[...], preferred_element_type=F32)
    hidden = (pre * jax.nn.sigmoid(pre)).astype(BF16)
    hid_keep[...] = hidden
    users[block_rows(me), :] = jnp.dot(hidden, w2_ref[...], preferred_element_type=F32).astype(BF16)
    items_all[z] = items_ref[...]
    meta_all[me] = meta_ref[...]

    pl.semaphore_wait(barrier, peers - 1 + 2)

    def z_forward(r):
        for way, sign in enumerate(signs):
            for half in (0, 1):
                length = chain_length(nz, way, half)
                rows = pl.ds(half * half_size, half_size)
                if 1 <= r <= length:
                    arrived(items_all.at[z_at(-sign * r), rows], z_recv.at[way, half, r - 1])
                if r < length:
                    block = z_at(-sign * r)
                    src = items_ref.at[rows] if r == 0 else items_all.at[block, rows]
                    send(src, items_all.at[block, rows], z_send.at[way, half, r],
                         z_recv.at[way, half, r], {"rows_0": z_at(sign)})

    def x_forward(r):
        for way, sign in enumerate(signs):
            for half in (0, 1):
                length = chain_length(nx, way, half)
                place = users.at[rows_of(x_at(-sign * r) * nc + c, half)]
                if 1 <= r <= length:
                    arrived(place, x_recv.at[way, half, r - 1])
                if r < length:
                    send(place, place, x_send.at[way, half, r], x_recv.at[way, half, r],
                         {"rows_1": x_at(sign)})
                if 1 <= r <= length:
                    send(place, place, p_send.at[way, half, r], p_recv.at[way, half, r], partner)
                if r == 0 and way == 0:
                    send(place, place, p_send.at[way, half, 0], p_recv.at[way, half, 0], partner)

    def from_partner():
        for way, sign in enumerate(signs):
            for half in (0, 1):
                for r in range(1 if way else 0, chain_length(nx, way, half) + 1):
                    place = users.at[rows_of(x_at(-sign * r) * nc + 1 - c, half)]
                    arrived(place, p_recv.at[way, half, r])

    x_forward(0)
    z_forward(0)
    for step in range(1, peers):
        send(meta_all.at[me], meta_all.at[me], m_send.at[step], m_recv.at[step], peer(step))

    pre_keep[...] = pre.T

    for r in range(1, nx // 2 + 1):
        x_forward(r)
        if r == 1:
            z_forward(1)
    from_partner()

    def first_pass(chunk):
        own = items_all[chunk]
        items_turned[:, block_rows(chunk)] = own.T

        @pl.loop(0, peers)
        def _(k):
            s = contract(items_all[chunk], users[block_rows(k), :], (1, 1))
            top = jnp.max(s, axis=0, keepdims=True)
            p = jnp.exp(s - top)
            probs[chunk * peers + k] = p
            peaks[chunk, pl.ds(k, 1), :] = top
            sums[chunk, pl.ds(k, 1), :] = jnp.sum(p, axis=0, keepdims=True)

    first_pass(z)
    for r in range(1, nz // 2 + 1):
        if r > 1:
            z_forward(r)
        if r < nz // 2:
            first_pass(z_at(r))
            first_pass(z_at(-r))
        else:
            first_pass(z_at(r))

    tops = peaks[...]
    top = jnp.max(tops, axis=0)
    lses[me] = top + jnp.log(jnp.sum(sums[...] * jnp.exp(tops - top[None]), axis=0))
    for step in range(1, peers):
        send(lses.at[me], lses.at[me], l_send.at[step], l_recv.at[step], peer(step))
    for step in range(1, peers):
        arrived(meta_all.at[from_peer(step)], m_recv.at[step])
    for step in range(1, peers):
        arrived(lses.at[from_peer(step)], l_recv.at[step])
    parts = lses[...]
    top = jnp.max(parts, axis=0)
    total = top + jnp.log(jnp.sum(jnp.exp(parts - top[None]), axis=0))
    scale[...] = jnp.exp(tops - total[None])

    lines = lax.broadcasted_iota(jnp.int32, (size, size), 0)

    def second_pass(chunk):
        first = ((chunk * nx + x) * nc + c) * size

        @pl.loop(0, peers)
        def _(k):
            weight = meta_all[k, 0:1, :]
            target = meta_all[k, 1:2, :].astype(jnp.int32) - first
            t = probs[chunk * peers + k] * (scale[chunk, pl.ds(k, 1), :] * weight)
            t = jnp.where(lines == target, t - weight, t)
            ds[block_rows(chunk), block_rows(k)] = t.astype(BF16)

        gi_part[chunk] = jnp.dot(ds[block_rows(chunk), :], users[...], preferred_element_type=F32)

    def z_reduce(r, parts_of=((0, 0), (0, 1), (1, 0), (1, 1))):
        for way, half in parts_of:
            sign = signs[way]
            length = chain_length(nz, way, half)
            rows = pl.ds(half * half_size, half_size)
            dest = z_at(sign * (length - r))
            if 1 <= r <= length:
                land = z_land.at[way, half, r - 1]
                arrived(land, zr_recv.at[way, half, r - 1])
                if r < length:
                    land[...] += gi_part[dest, rows]
            if r < length:
                src = gi_part.at[dest, rows] if r == 0 else z_land.at[way, half, r - 1]
                send(src, z_land.at[way, half, r], zr_send.at[way, half, r],
                     zr_recv.at[way, half, r], {"rows_0": z_at(sign)})

    second_pass(z_at(nz // 2))
    z_reduce(0, ((0, 0), (1, 1)))
    second_pass(z_at(nz // 2 - 1))
    z_reduce(0, ((0, 1),))
    second_pass(z_at(1 - nz // 2))
    z_reduce(0, ((1, 0),))
    for r in range(nz // 2 - 2, 0, -1):
        second_pass(z_at(r))
        second_pass(z_at(-r))
    second_pass(z)

    def user_pass(k):
        gu_part[k] = jnp.dot(items_turned[...], ds[:, block_rows(k)], preferred_element_type=F32)

    z_reduce(1)
    for step in range(nx):
        k = x_at(step) * nc + 1 - c
        user_pass(k)
        send(gu_part.at[k], gu_pair.at[x_at(step)], d_send.at[step], d_recv.at[step], partner)
    for step in range(nx):
        user_pass(x_at(step) * nc + c)
    for step in range(nx):
        arrived(gu_pair.at[x_at(step)], d_recv.at[step])
        gu_pair[x_at(step)] += gu_part[x_at(step) * nc + c]

    def x_reduce(r):
        for way, sign in enumerate(signs):
            for half in (0, 1):
                length = chain_length(nx, way, half)
                rows = pl.ds(half * half_size, half_size)
                dest = x_at(sign * (length - r))
                if 1 <= r <= length:
                    land = x_land.at[way, half, r - 1]
                    arrived(land, xr_recv.at[way, half, r - 1])
                    if r < length:
                        land[...] += gu_pair[dest, rows]
                if r < length:
                    src = gu_pair.at[dest, rows] if r == 0 else x_land.at[way, half, r - 1]
                    send(src, x_land.at[way, half, r], xr_send.at[way, half, r],
                         xr_recv.at[way, half, r], {"rows_1": x_at(sign)})

    x_reduce(0)
    for r in range(1, nx // 2 + 1):
        if r + 1 <= nz // 2:
            z_reduce(r + 1)
        x_reduce(r)

    def collected(own, land, n):
        pieces = []
        for half in (0, 1):
            got = own[half * half_size : (half + 1) * half_size]
            for way in (0, 1):
                length = chain_length(n, way, half)
                if length:
                    got = got + land[way, half, length - 1]
            pieces.append(got)
        return jnp.concatenate(pieces, axis=0)

    gu = collected(gu_pair[x], x_land, nx).astype(BF16)
    pre = pre_keep[...]
    gate = jax.nn.sigmoid(pre)
    back = jnp.dot(w2_ref[...], gu, preferred_element_type=F32)
    grad_pre = (back * gate * (1.0 + pre * (1.0 - gate))).astype(BF16)
    df_ref[0] = jnp.dot(grad_pre, feat_ref[...], preferred_element_type=F32)
    df_ref[1] = jnp.dot(gu, hid_keep[...], preferred_element_type=F32)

    for r in range(nx // 2 + 2, nz // 2 + 1):
        z_reduce(r)
    gi_ref[...] = collected(gi_part[z], z_land, nz)
    for copy in pending:
        copy.wait_send()


def block_grads(features, w_first, w_second, items, meta):
    nz, nx, nc = (lax.axis_size(a) for a in ("rows_0", "rows_1", "rows_2"))
    size, width = items.shape
    peers = nx * nc
    vmem, dma = pltpu.VMEM, pltpu.SemaphoreType.DMA
    zh, xh = nz // 2, nx // 2
    return pl.pallas_call(
        functools.partial(block_kernel, nz, nx, nc),
        out_shape=(
            jax.ShapeDtypeStruct((size, width), F32),
            jax.ShapeDtypeStruct((2, width, width), F32),
        ),
        in_specs=[pl.BlockSpec(memory_space=vmem)] * 5,
        out_specs=[pl.BlockSpec(memory_space=vmem)] * 2,
        scratch_shapes=[
            vmem((peers * size, width), BF16),
            vmem((nz, size, width), BF16),
            vmem((width, nz * size), BF16),
            vmem((peers, 2, size), F32),
            vmem((nz, peers, size), F32),
            vmem((nz, peers, size), F32),
            vmem((peers, peers, size), F32),
            vmem((nz, peers, size), F32),
            vmem((nz * peers, size, size), F32),
            vmem((nz * size, peers * size), BF16),
            vmem((nz, size, width), F32),
            vmem((peers, width, size), F32),
            vmem((nx, width, size), F32),
            vmem((2, 2, zh, size // 2, width), F32),
            vmem((2, 2, xh, width // 2, size), F32),
            vmem((width, size), F32),
            vmem((size, width), BF16),
            dma((2, 2, zh)), dma((2, 2, zh)),
            dma((2, 2, xh)), dma((2, 2, xh)),
            dma((2, 2, xh + 1)), dma((2, 2, xh + 1)),
            dma((peers,)), dma((peers,)),
            dma((peers,)), dma((peers,)),
            dma((2, 2, zh)), dma((2, 2, zh)),
            dma((nx,)), dma((nx,)),
            dma((2, 2, xh)), dma((2, 2, xh)),
        ],
        compiler_params=pltpu.CompilerParams(
            collective_id=0, has_side_effects=True, vmem_limit_bytes=60 * 2**20
        ),
        cost_estimate=pl.CostEstimate(flops=7 * 10**9, bytes_accessed=2**20, transcendentals=2**22),
        name="block_grads",
    )(features, w_first, w_second, items, meta)


def cut_along(value, dim, count):
    before, after = (value.shape[:dim], value.shape[dim + 1 :])
    return jnp.moveaxis(value.reshape(*before, count, -1, *after), dim, 0)


def sum_at_owner(value, axis, dim):
    count = lax.axis_size(axis)
    tiles = lax.all_to_all(cut_along(value, dim, count), axis, 0, 0, tiled=True)
    return jnp.sum(tiles, axis=0)


def summed_rows(value, axes, dim):
    far, near = axes
    tiles = cut_along(value, dim, lax.axis_size(far))
    nearer = sum_at_owner(tiles, near, dim + 1)
    arrived = lax.all_to_all(nearer, far, split_axis=0, concat_axis=0, tiled=True)
    return arrived.sum(axis=0)


def padded_to(lines, count):
    spare = -lines.shape[0] % count
    if not spare:
        return lines
    return jnp.concatenate([lines, jnp.zeros((spare, *lines.shape[1:]), lines.dtype)])


def sent_to_all(value, axis):
    count = lax.axis_size(axis)
    return lax.all_to_all(
        jnp.broadcast_to(value[None], (count, *value.shape)), axis, 0, 0, tiled=True
    )


def joined_along(tiles, dim):
    shape = list(tiles.shape[1:])
    shape[dim] *= tiles.shape[0]
    return jnp.moveaxis(tiles, 0, dim).reshape(shape)


def gather_axes(value, axes, dim):
    far, near = axes
    tiles = sent_to_all(sent_to_all(value, far), near)
    return joined_along(tiles.swapaxes(0, 1).reshape(-1, *value.shape), dim)


def total_of(value, axes):
    own = summed_rows(padded_to(value, lax.axis_size(axes[0]) * lax.axis_size(axes[1])), axes, 0)
    whole = gather_axes(own, axes, 0)
    return whole[: len(value)].reshape(value.shape)


def in_one(arrays, axis):
    flat, at, done = (jnp.concatenate([a.reshape(-1) for a in arrays]), 0, [])
    total = total_of(flat, axis)
    for a in arrays:
        done.append(total[at : at + a.size].reshape(a.shape))
        at += a.size
    return tuple(done)


def one_exchange(value, axis, axes, splits, concats):
    sizes = [lax.axis_size(a) for a in axes]
    tiles = cut_along(value, splits[0], sizes[0])
    tiles = jnp.moveaxis(cut_along(tiles, splits[1] + 1, sizes[1]), 0, 1)
    inside = tiles.shape[2:]
    tiles = tiles.reshape(-1, *inside)
    tiles = lax.all_to_all(tiles, axis, split_axis=0, concat_axis=0, tiled=True)
    tiles = joined_along(tiles.reshape(*sizes, *inside), concats[0] + 1)
    return joined_along(tiles, concats[1])


def body(
    user_features, w_first, w_second, item_embed, example_weight, positive, item_owner, item_row
):
    own_items = item_embed[0]
    owners = item_owner[0, :, 0]
    item_rows = item_row[0]
    my_users, feature_width = own_items.shape
    peers = lax.axis_size(ROWS)
    groups = lax.axis_size("grp")
    capacity = max(2, 4 * my_users // peers)
    member = (owners[:, None] == lax.broadcasted_iota(jnp.int32, (1, peers), 1)).astype(jnp.int32)
    before = jnp.cumsum(member, axis=0) - member
    slot_rank = jnp.sum(before * member, axis=1)
    slots = owners * capacity + slot_rank
    send_rows = (
        jnp.full((peers * capacity,), -1.0, F32).at[slots].set(item_rows.astype(F32))
    )
    rows_wide = jnp.broadcast_to(send_rows.reshape(peers, capacity, 1), (peers, capacity, groups))
    got_rows = one_exchange(rows_wide, ROWS_GRP, (ROWS, "grp"), (0, 2), (0, 1))
    meta = jnp.stack([example_weight[0], positive[0].astype(F32)])
    grad_item, tower = block_grads(user_features[0], w_first, w_second, own_items, meta)
    send_grad = jnp.zeros((peers * capacity, feature_width), BF16).at[slots].set(grad_item.astype(BF16))
    send_grad = send_grad.reshape(peers, capacity, feature_width)
    got_grad = one_exchange(send_grad, ROWS_GRP, (ROWS, "grp"), (0, 2), (0, 1))
    (summed,) = in_one((tower,), (("rows_0", "rows_1"), ("rows_2", "grp")))
    share_width = feature_width // groups
    table_rows = got_rows.reshape(-1).astype(jnp.int32)
    table_rows = jnp.where(table_rows >= 0, table_rows, ITEMS_DEV)
    grad_table = (
        jnp.zeros((ITEMS_DEV, share_width), F32)
        .at[table_rows]
        .add(got_grad.reshape(-1, share_width).astype(F32), mode="drop")
    )
    return (summed[0].T, summed[1].T, grad_table)


def solution(mesh):
    torus = Mesh(
        mesh.devices.reshape(8, 4, 2, mesh.shape["grp"]), ("rows_0", "rows_1", "rows_2", "grp")
    )
    placed = (
        P("grp", ROWS, None),
        P(),
        P(),
        P("grp", ROWS, None),
        P("grp", ROWS),
        P("grp", ROWS),
        P("grp", ROWS, None),
        P("grp", ROWS),
    )
    return jax.shard_map(
        body, mesh=torus, in_specs=placed, out_specs=(P(), P(), P(ROWS, "grp")), check_vma=False
    )
```

time: 338 us -> 201 us (0.59)
  waiting for transfers between devices: 130 us -> 53.4 us
  Pallas kernels: 0 us -> 70.3 us
  matrix products: 48 us -> 0 us
  blocking collectives: 45.7 us -> 0 us
  between operations: 14.3 us -> 0.86 us
  other arithmetic: 37.8 us -> 27.5 us
  starting transfers between devices: 41.3 us -> 34.1 us
  local copies, waits for them, and re-layouts: 20.6 us -> 14.3 us
    all_gather x2 -> x0, waiting for transfers between devices: 84.9 us -> none  [the longest x1 84.9 us: body(): gathered = lax.all_gather(own_items, ROWS, axis=0, tiled=True)]
    pallas_call x0 -> x1, Pallas kernels: none -> 70.3 us  [block_grads(): pl.pallas_call(functools.partial(block_kernel, nz, nx, nc), out_shape=(ja...]
    dot_general x8 -> x0, matrix products: 48 us -> none  [the longest x2 24.1 us: contract_last(): lax.dot_general(left, right, (((1,), (1,)), ((), ())), preferred_element_...]
    all_gather x1 -> x0, blocking collectives: 45.7 us -> none  [gather_turned(): filled = lax.all_gather(both, axis, axis=0, tiled=True)]
    reduce_sum x1 -> x0, other arithmetic: 8.27 us -> none  [body(): jnp.sum(jnp.exp(scores - row_max), axis=1, keepdims=True)]
    all_to_all x1, waiting for transfers between devices: 0.01 us -> 7.32 us  [summed_rows(): lax.all_to_all(nearer, far, split_axis=0, concat_axis=0, tiled=True)]
    all_to_all x2, starting transfers between devices: 18.9 us -> 13.8 us  [one_exchange(): tiles = lax.all_to_all(tiles, axis, split_axis=0, concat_axis=0, tiled=True)]
    all_to_all x2, starting transfers between devices: 12.7 us -> 7.95 us  [sent_to_all(): lax.all_to_all(jnp.broadcast_to(value[None], (count, *value.shape)), axis...]
  transfers between devices with their start and end apart: 8 -> 6, of which waited for: 5 -> 5; matrix products, arithmetic and copies ran while one was open for 22% -> 16% of each run, Pallas kernels for 0% -> 0%
where the time goes in v1:
time: 201 us; the launch traced here: 200 us
  Pallas kernels  70.3 us (35%)
  waiting for transfers between devices  53.4 us (27%)
  starting transfers between devices  34.1 us (17%)
  other arithmetic  27.5 us (14%)
  local copies, waits for them, and re-layouts  14.3 us (7%)
    pallas_call x1, Pallas kernels, block_grads(): pl.pallas_call(functools.partial(block_kernel, nz, nx, nc), out_shape=(ja...  70.3 us
    all_to_all x2, waiting for transfers between devices, one_exchange(): tiles = lax.all_to_all(tiles, axis, split_axis=0, concat_axis=0, tiled=True)  32.5 us
    scatter-add x1, other arithmetic, body(): grad_table = jnp.zeros((ITEMS_DEV, share_width), F32).at[table_rows].add(...  22.9 us
    all_to_all x2, starting transfers between devices, one_exchange(): tiles = lax.all_to_all(tiles, axis, split_axis=0, concat_axis=0, tiled=True)  13.8 us
    all_to_all x1, waiting for transfers between devices, sum_at_owner(): tiles = lax.all_to_all(cut_along(value, dim, count), axis, 0, 0, tiled=True)  8.35 us
    all_to_all x2, starting transfers between devices, sent_to_all(): lax.all_to_all(jnp.broadcast_to(value[None], (count, *value.shape)), axis...  7.95 us
    all_to_all x1, waiting for transfers between devices, summed_rows(): lax.all_to_all(nearer, far, split_axis=0, concat_axis=0, tiled=True)  7.32 us
    all_to_all x1, starting transfers between devices, sum_at_owner(): tiles = lax.all_to_all(cut_along(value, dim, count), axis, 0, 0, tiled=True)  6.34 us
  transfers between devices with their start and end apart: 6, of which 5 were waited for; matrix products, arithmetic and copies ran while one was open for 16% of the time, Pallas kernels for 0%

profile of v1, /device:TPU:1, one launch (start us, length us, event | category | flops | bytes accessed | tf_op | source)
XLA Modules:
  0.0 200.5 jit_solution(8687159563902805052)
XLA Ops:
  1.3 1.3 pad_maximum_fusion.meta_ref
  2.6 70.3 %block_grads.1 = (f32[256,256]{1,0:T(8,128)}, f32[2,256,256]{2,1,0:T(8,128)}) custom-call(bf16[256,256]{1,0:T(8,128)(2,1)} %bitcast.82, bf16[256,256]{1,0:T(8,128)(2,1)} %w1_ref.1, bf16[256,256]{1,0:T(8,128)(2,1)} %w2_ref.1, bf16[256,256]{1,0:T(8,128)(2,1)} %bitcast.83, f32[2,256]{1,0:T(2,128)} %pad_maximum_fusion.meta_ref), custom_call_target="tpu_custom_call" | custom-call | flops 7000000000 | bytes 1048576 | tf_op jit(solution)/shard_map/block_grads/pallas_call | solution.py:286
  72.9 1.2 reshape_reshape_reshape.7
  74.1 1.1 copy.34
  75.2 6.3 %all-to-all-start = ((f32[8,32,512]{2,1,0:T(8,128)}), f32[8,32,512]{2,1,0:T(8,128)S(1)}, u32[]{:S(2)}, u32[]{:S(2)}) async-start(f32[8,32,512]{2,1,0:T(8,128)} %bitcast.64), calls=%async_computation | async-start | bytes 1048576 | tf_op jit(solution)/shard_map/all_to_all | solution.py:336
  82.5 8.4 %all-to-all-done = f32[8,32,512]{2,1,0:T(8,128)S(1)} async-done(((f32[8,32,512]{2,1,0:T(8,128)}), f32[8,32,512]{2,1,0:T(8,128)S(1)}, u32[]{:S(2)}, u32[]{:S(2)}) %all-to-all-start) | async-done | bytes 524320 | tf_op jit(solution)/shard_map/all_to_all | solution.py:336
  91.6 6.0 %all-to-all-start.1 = ((f32[32,1,512]{2,1,0:T(1,128)}), f32[32,1,512]{2,1,0:T(1,128)S(1)}, u32[]{:S(2)}, u32[]{:S(2)}) async-start(f32[32,1,512]{2,1,0:T(1,128)} %all_to_all.23), calls=%async_computation.1 | async-start | bytes 131072 | tf_op jit(solution)/shard_map/all_to_all | solution.py:344
  97.7 1.4 scatter_custom_fusion
  99.2 7.3 %all-to-all-done.1 = f32[32,1,512]{2,1,0:T(1,128)S(1)} async-done(((f32[32,1,512]{2,1,0:T(1,128)}), f32[32,1,512]{2,1,0:T(1,128)S(1)}, u32[]{:S(2)}, u32[]{:S(2)}) %all-to-all-start.1) | async-done | bytes 65568 | tf_op jit(solution)/shard_map/all_to_all | solution.py:344
  107.2 6.9 %all-to-all-start.4 = ((f32[256,1,16,1]{2,3,1,0:T(1,128)}), f32[256,1,16,1]{2,3,1,0:T(1,128)S(1)}, u32[]{:S(2)}, u32[]{:S(2)}) async-start(f32[256,1,16,1]{2,3,1,0:T(1,128)} %bitcast.13), calls=%async_computation.4 | async-start | bytes 262144 | tf_op jit(solution)/shard_map/all_to_all | solution.py:395
  114.1 12.7 %all-to-all-done.4 = f32[256,1,16,1]{2,3,1,0:T(1,128)S(1)} async-done(((f32[256,1,16,1]{2,3,1,0:T(1,128)}), f32[256,1,16,1]{2,3,1,0:T(1,128)S(1)}, u32[]{:S(2)}, u32[]{:S(2)}) %all-to-all-start.4) | async-done | bytes 16416 | tf_op jit(solution)/shard_map/all_to_all | solution.py:395
  127.5 3.9 %all-to-all-start.2 = ((f32[32,1,512]{2,1,0:T(1,128)}), f32[32,1,512]{2,1,0:T(1,128)S(1)}, u32[]{:S(2)}, u32[]{:S(2)}) async-start(f32[32,1,512]{2,1,0:T(1,128)} %broadcast_in_dim.18), calls=%async_computation.2 | async-start | bytes 131072 | tf_op jit(solution)/shard_map/all_to_all | solution.py:357
  131.4 1.6 scatter_custom_fusion.1
  133.8 1.3 reshape.153
  135.1 5.2 %all-to-all-done.2 = f32[32,1,512]{2,1,0:T(1,128)S(1)} async-done(((f32[32,1,512]{2,1,0:T(1,128)}), f32[32,1,512]{2,1,0:T(1,128)S(1)}, u32[]{:S(2)}, u32[]{:S(2)}) %all-to-all-start.2) | async-done | bytes 65568 | tf_op jit(solution)/shard_map/all_to_all | solution.py:357
  140.3 6.9 %all-to-all-start.5 = ((bf16[256,2,512]{2,1,0:T(2,128)(2,1)}), bf16[256,2,512]{2,1,0:T(2,128)(2,1)S(1)}, u32[]{:S(2)}, u32[]{:S(2)}) async-start(bf16[256,2,512]{2,1,0:T(2,128)(2,1)} %reshape.153), calls=%async_computation.5 | async-start | bytes 1048576 | tf_op jit(solution)/shard_map/all_to_all | solution.py:395
  147.5 19.7 %all-to-all-done.5 = bf16[256,2,512]{2,1,0:T(2,128)(2,1)S(1)} async-done(((bf16[256,2,512]{2,1,0:T(2,128)(2,1)}), bf16[256,2,512]{2,1,0:T(2,128)(2,1)S(1)}, u32[]{:S(2)}, u32[]{:S(2)}) %all-to-all-start.5) | async-done | bytes 524320 | tf_op jit(solution)/shard_map/all_to_all | solution.py:395
  167.2 0.9 broadcast_in_dim.37
  168.1 4.1 %all-to-all-start.3 = ((f32[8,32,512]{2,1,0:T(8,128)}), f32[8,32,512]{2,1,0:T(8,128)}, u32[]{:S(2)}, u32[]{:S(2)}) async-start(f32[8,32,512]{2,1,0:T(8,128)} %broadcast_in_dim.37), calls=%async_computation.3 | async-start | bytes 1048576 | tf_op jit(solution)/shard_map/all_to_all | solution.py:357
  172.8 22.9 %scatter_custom_fusion.2 = f32[4096,64]{1,0:T(8,128)S(1)} fusion(s32[4096]{0:T(1024)S(1)} %bitcast.75, bf16[4096,64]{1,0:T(8,128)(2,1)S(1)} %bitcast.68, f32[]{:T(128)} %constant.7.clone.1), kind=kCustom, calls=%fused_computation.3 | custom fusion | flops 524288 | bytes 2097156 | tf_op jit(solution)/shard_map/scatter-add | solution.py:431
  195.7 1.6 copy.28
  197.3 1.1 fusion.12
  198.6 0.8 copy.27
  199.6 0.8 copy.26
  (33 shorter events, 5.8 us)
Async XLA Ops:
  72.9 8.7 %copy-start.2 = (s32[1,256]{1,0:T(1,128)S(1)}, s32[1,256]{1,0:T(1,128)}, u32[]{:S(2)}) copy-start(s32[1,256]{1,0:T(1,128)} %param.15) | copy-start | bytes 3076
  72.9 8.7 %copy-start.1 = (s32[1,256,1]{1,2,0:T(1,128)S(1)}, s32[1,256,1]{1,2,0:T(1,128)}, u32[]{:S(2)}) copy-start(s32[1,256,1]{1,2,0:T(1,128)} %param.14) | copy-start | bytes 3076
  74.1 57.3 %copy-start = (f32[256,256]{1,0:T(8,128)S(1)}, f32[256,256]{1,0:T(8,128)}, u32[]{:S(2)}) copy-start(f32[256,256]{1,0:T(8,128)} %get-tuple-element.6) | copy-start | bytes 786436
  75.2 15.7 %all-to-all-start = ((f32[8,32,512]{2,1,0:T(8,128)}), f32[8,32,512]{2,1,0:T(8,128)S(1)}, u32[]{:S(2)}, u32[]{:S(2)}) async-start(f32[8,32,512]{2,1,0:T(8,128)} %bitcast.64), calls=%async_computation | async-start | bytes 1048576 | tf_op jit(solution)/shard_map/all_to_all | solution.py:336
  91.6 14.9 %all-to-all-start.1 = ((f32[32,1,512]{2,1,0:T(1,128)}), f32[32,1,512]{2,1,0:T(1,128)S(1)}, u32[]{:S(2)}, u32[]{:S(2)}) async-start(f32[32,1,512]{2,1,0:T(1,128)} %all_to_all.23), calls=%async_computation.1 | async-start | bytes 131072 | tf_op jit(solution)/shard_map/all_to_all | solution.py:344
  107.2 19.7 %all-to-all-start.4 = ((f32[256,1,16,1]{2,3,1,0:T(1,128)}), f32[256,1,16,1]{2,3,1,0:T(1,128)S(1)}, u32[]{:S(2)}, u32[]{:S(2)}) async-start(f32[256,1,16,1]{2,3,1,0:T(1,128)} %bitcast.13), calls=%async_computation.4 | async-start | bytes 262144 | tf_op jit(solution)/shard_map/all_to_all | solution.py:395
  127.5 12.8 %all-to-all-start.2 = ((f32[32,1,512]{2,1,0:T(1,128)}), f32[32,1,512]{2,1,0:T(1,128)S(1)}, u32[]{:S(2)}, u32[]{:S(2)}) async-start(f32[32,1,512]{2,1,0:T(1,128)} %broadcast_in_dim.18), calls=%async_computation.2 | async-start | bytes 131072 | tf_op jit(solution)/shard_map/all_to_all | solution.py:357
  140.3 26.9 %all-to-all-start.5 = ((bf16[256,2,512]{2,1,0:T(2,128)(2,1)}), bf16[256,2,512]{2,1,0:T(2,128)(2,1)S(1)}, u32[]{:S(2)}, u32[]{:S(2)}) async-start(bf16[256,2,512]{2,1,0:T(2,128)(2,1)} %reshape.153), calls=%async_computation.5 | async-start | bytes 1048576 | tf_op jit(solution)/shard_map/all_to_all | solution.py:395
  168.1 29.3 %all-to-all-start.3 = ((f32[8,32,512]{2,1,0:T(8,128)}), f32[8,32,512]{2,1,0:T(8,128)}, u32[]{:S(2)}, u32[]{:S(2)}) async-start(f32[8,32,512]{2,1,0:T(8,128)} %broadcast_in_dim.37), calls=%async_computation.3 | async-start | bytes 1048576 | tf_op jit(solution)/shard_map/all_to_all | solution.py:357

commit v2 on v1

--- a/solution.py
+++ b/solution.py
@@ -9,7 +9,6 @@
 
 ITEMS_DEV = 4096
 ROWS = ("rows_0", "rows_1", "rows_2")
-ROWS_GRP = ("rows_0", "rows_1", "rows_2", "grp")
 MESH = pl.DeviceIdType.MESH
 F32 = jnp.float32
 BF16 = jnp.bfloat16
@@ -24,13 +23,19 @@
 
 
 def block_kernel(
-    nz, nx, nc, feat_ref, w1_ref, w2_ref, items_ref, meta_ref, gi_ref, df_ref,
+    nz, nx, nc, ny, feat_ref, w1_ref, w2_ref, items_ref, meta_ref, pairs_ref, got_ref, ids_ref, tower_ref,
     users, items_all, items_turned, meta_all, peaks, sums, lses, scale, probs, ds,
     gi_part, gu_part, gu_pair, z_land, x_land, pre_keep, hid_keep,
     z_send, z_recv, x_send, x_recv, p_send, p_recv, m_send, m_recv, l_send, l_recv,
     zr_send, zr_recv, d_send, d_recv, xr_send, xr_recv,
+    pairs_all, slots_keep, ids_out, share_out, share_in, slotted,
+    df_keep, df_pair, y_part, y_land, p_part, p_land,
+    i_send, i_recv, n_send, n_recv, s_send, s_recv, e_send, e_recv,
+    ac_send, ac_recv, ay_send, ay_recv, ap_send, ap_recv,
+    gp_send, gp_recv, gy_send, gy_recv, gc_send, gc_recv,
 ):
     z, x, c = lax.axis_index("rows_0"), lax.axis_index("rows_1"), lax.axis_index("rows_2")
+    y = lax.axis_index("grp")
     size = items_ref.shape[0]
     half_size = size // 2
     peers = nx * nc
@@ -66,12 +71,45 @@
         pltpu.make_async_copy(ref, ref, recv_sem).wait()
 
     barrier = pltpu.get_barrier_semaphore()
-    for step in range(1, peers):
-        pl.semaphore_signal(barrier, inc=1, device_id=peer(step), device_id_type=MESH)
-    for sign in signs:
-        pl.semaphore_signal(
-            barrier, inc=1, device_id={"rows_0": z_at(sign)}, device_id_type=MESH
-        )
+    plane = nz * peers
+    here = z * peers + me
+    tiles = nz * nx
+    tile = z * nx + x
+
+    def far(step):
+        to_z = lax.rem(z + step // peers, nz)
+        to_x = lax.rem(x + (step % peers) // nc, nx)
+        to_c = lax.rem(c + step % nc, nc)
+        return {"rows_0": to_z, "rows_1": to_x, "rows_2": to_c}, (to_z * nx + to_x) * nc + to_c
+
+    def from_far(step):
+        of_z = lax.rem(z + nz - step // peers, nz)
+        of_x = lax.rem(x + nx - (step % peers) // nc, nx)
+        of_c = lax.rem(c + nc - step % nc, nc)
+        return (of_z * nx + of_x) * nc + of_c
+
+    def far_tile(step):
+        to_z, to_x = lax.rem(z + step // nx, nz), lax.rem(x + step % nx, nx)
+        return {"rows_0": to_z, "rows_1": to_x}, to_z * nx + to_x
+
+    def from_far_tile(step):
+        return lax.rem(z + nz - step // nx, nz) * nx + lax.rem(x + nx - step % nx, nx)
+
+    def y_at(step):
+        return lax.rem(y + step + ny, ny)
+
+    def send_plainly(src, dst, send_sem, recv_sem, where):
+        pltpu.make_async_remote_copy(
+            src_ref=src, dst_ref=dst, send_sem=send_sem, recv_sem=recv_sem,
+            device_id=where, device_id_type=MESH,
+        ).start()
+
+    @pl.loop(1, plane)
+    def _(step):
+        pl.semaphore_signal(barrier, inc=1, device_id=far(step)[0], device_id_type=MESH)
+
+    for step in range(1, ny):
+        pl.semaphore_signal(barrier, inc=1, device_id={"grp": y_at(step)}, device_id_type=MESH)
 
     def rows_of(block, half):
         return pl.ds(pl.multiple_of(block * size + half * half_size, half_size), half_size)
@@ -86,7 +124,8 @@
     items_all[z] = items_ref[...]
     meta_all[me] = meta_ref[...]
 
-    pl.semaphore_wait(barrier, peers - 1 + 2)
+    pairs_all[y] = pairs_ref[...]
+    pl.semaphore_wait(barrier, plane - 1 + ny - 1)
 
     def z_forward(r):
         for way, sign in enumerate(signs):
@@ -128,12 +167,52 @@
     for step in range(1, peers):
         send(meta_all.at[me], meta_all.at[me], m_send.at[step], m_recv.at[step], peer(step))
 
+    for step in range(1, ny):
+        send(pairs_all.at[y], pairs_all.at[y], i_send.at[step], i_recv.at[step],
+             {"grp": y_at(step)})
+
     pre_keep[...] = pre.T
+
+    cap = got_ref.shape[2]
+    share = got_ref.shape[3] // 2
+
+    def name_slots():
+        earlier = (
+            lax.broadcasted_iota(jnp.int32, (size, size), 0)
+            < lax.broadcasted_iota(jnp.int32, (size, size), 1)
+        ).astype(BF16)
+        owner_lines = lax.broadcasted_iota(jnp.int32, (plane, size), 0)
+        rank_lines = lax.broadcasted_iota(jnp.int32, (cap, size), 0)
+        pieces, most = [], None
+        for g in range(ny):
+            owner = pairs_all[g, 0:1, :].astype(jnp.int32)
+            row = pairs_all[g, 1:2, :]
+            member = (owner_lines == owner).astype(F32)
+            before = jnp.dot(member.astype(BF16), earlier, preferred_element_type=F32)
+            rank = jnp.sum(before * member, axis=0, keepdims=True).astype(jnp.int32)
+            slots_keep[g] = owner * cap + rank
+            at_rank = (rank_lines == rank).astype(BF16)
+            high = jnp.floor(row * (1.0 / 64.0))
+            low = row - 64.0 * high
+            found = contract(member.astype(BF16), at_rank, (1, 1))
+            ids = 64.0 * contract((member * high).astype(BF16), at_rank, (1, 1)) + contract(
+                (member * low).astype(BF16), at_rank, (1, 1)
+            )
+            pieces.append(jnp.where(found > 0.5, ids, float(ITEMS_DEV)))
+            count = jnp.sum(member, axis=1, keepdims=True)
+            most = count if most is None else jnp.maximum(most, count)
+        spare = ids_ref.shape[2] - ny * cap
+        pieces.append(jnp.broadcast_to(most, (plane, spare)))
+        named = jnp.concatenate(pieces, axis=1).astype(jnp.int32)
+        ids_out[...] = named.reshape(ids_out.shape)
 
     for r in range(1, nx // 2 + 1):
         x_forward(r)
         if r == 1:
             z_forward(1)
+            for step in range(1, ny):
+                arrived(pairs_all.at[y_at(-step)], i_recv.at[step])
+            name_slots()
     from_partner()
 
     def first_pass(chunk):
@@ -150,6 +229,13 @@
             sums[chunk, pl.ds(k, 1), :] = jnp.sum(p, axis=0, keepdims=True)
 
     first_pass(z)
+
+    @pl.loop(1, plane)
+    def _(step):
+        where, there = far(step)
+        send_plainly(ids_out.at[there], ids_ref.at[here], n_send.at[step], n_recv.at[step], where)
+
+    ids_ref[here] = ids_out[here]
     for r in range(1, nz // 2 + 1):
         if r > 1:
             z_forward(r)
@@ -267,30 +353,129 @@
     gate = jax.nn.sigmoid(pre)
     back = jnp.dot(w2_ref[...], gu, preferred_element_type=F32)
     grad_pre = (back * gate * (1.0 + pre * (1.0 - gate))).astype(BF16)
-    df_ref[0] = jnp.dot(grad_pre, feat_ref[...], preferred_element_type=F32)
-    df_ref[1] = jnp.dot(gu, hid_keep[...], preferred_element_type=F32)
+    df_keep[0] = jnp.dot(grad_pre, feat_ref[...], preferred_element_type=F32)
+    df_keep[1] = jnp.dot(gu, hid_keep[...], preferred_element_type=F32)
+
+    send(df_keep.at[1 - c], df_pair, ac_send, ac_recv, partner)
+    arrived(df_pair, ac_recv)
+    y_part[...] = (df_keep[c] + df_pair[...]).reshape(y_part.shape)
+    for step in range(1, ny):
+        send(y_part.at[y_at(step)], y_land.at[step - 1], ay_send.at[step], ay_recv.at[step],
+             {"grp": y_at(step)})
 
     for r in range(nx // 2 + 2, nz // 2 + 1):
         z_reduce(r)
-    gi_ref[...] = collected(gi_part[z], z_land, nz)
+    gi = collected(gi_part[z], z_land, nz).astype(BF16)
+
+    for to in range(ny):
+        cols = slice(to * share, (to + 1) * share)
+        share_out[to] = jnp.concatenate([gi[:half_size, cols], gi[half_size:, cols]], axis=1)
+    for step in range(1, ny):
+        send(share_out.at[y_at(step)], share_in.at[y], s_send.at[step], s_recv.at[step],
+             {"grp": y_at(step)})
+    share_in[y] = share_out[y]
+
+    whole = y_part[y]
+    for step in range(1, ny):
+        arrived(y_land.at[step - 1], ay_recv.at[step])
+        whole = whole + y_land[step - 1]
+    p_part[...] = whole.reshape(p_part.shape)
+
+    @pl.loop(1, tiles)
+    def _(step):
+        where, there = far_tile(step)
+        send_plainly(p_part.at[there], p_land.at[step], ap_send.at[step], ap_recv.at[step], where)
+
+    for step in range(1, ny):
+        arrived(share_in.at[y_at(-step)], s_recv.at[step])
+    slot_lines = lax.broadcasted_iota(jnp.int32, (plane * cap, size), 0)
+    for pair in range(ny // 2):
+        sides = []
+        for g in (2 * pair, 2 * pair + 1):
+            chosen = (slot_lines == slots_keep[g]).astype(BF16)
+            packed = share_in[g]
+            data = jnp.concatenate([packed[:, :share], packed[:, share:]], axis=0)
+            sides.append(jnp.dot(chosen, data, preferred_element_type=F32))
+        both = jnp.concatenate(sides, axis=1).astype(BF16)
+        slotted[:, pair] = both.reshape(plane, cap, 2 * share)
+    got_ref[here] = slotted[here]
+
+    def exchange(first, last):
+        @pl.loop(first, last)
+        def _(step):
+            where, there = far(step)
+            send_plainly(slotted.at[there], got_ref.at[here], e_send.at[step], e_recv.at[step],
+                         where)
+
+    exchange(1, plane // 2)
+    p_land[0] = p_part[tile]
+
+    @pl.loop(1, tiles)
+    def _(step):
+        arrived(p_land.at[step], ap_recv.at[step])
+
+    own = tower_ref.at[c, y, tile]
+    own[...] = jnp.sum(p_land[...], axis=0)
+
+    @pl.loop(1, tiles)
+    def _(step):
+        where, _ = far_tile(step)
+        send_plainly(own, own, gp_send.at[step], gp_recv.at[step], where)
+
+    exchange(plane // 2, plane)
+
+    @pl.loop(1, tiles)
+    def _(step):
+        arrived(tower_ref.at[c, y, from_far_tile(step)], gp_recv.at[step])
+
+    for step in range(1, ny):
+        send(tower_ref.at[c, y], tower_ref.at[c, y], gy_send.at[step], gy_recv.at[step],
+             {"grp": y_at(step)})
+    for step in range(1, ny):
+        arrived(tower_ref.at[c, y_at(-step)], gy_recv.at[step])
+    send(tower_ref.at[c], tower_ref.at[c], gc_send, gc_recv, partner)
+
+    @pl.loop(1, plane)
+    def _(step):
+        arrived(ids_ref.at[from_far(step)], n_recv.at[step])
+        arrived(got_ref.at[from_far(step)], e_recv.at[step])
+
+    arrived(tower_ref.at[1 - c], gc_recv)
     for copy in pending:
         copy.wait_send()
 
-
-def block_grads(features, w_first, w_second, items, meta):
-    nz, nx, nc = (lax.axis_size(a) for a in ("rows_0", "rows_1", "rows_2"))
+    @pl.loop(1, plane)
+    def _(step):
+        arrived(ids_out.at[0], n_send.at[step])
+        arrived(slotted.at[0], e_send.at[step])
+
+    @pl.loop(1, tiles)
+    def _(step):
+        arrived(p_part.at[0], ap_send.at[step])
+        arrived(p_part.at[0], gp_send.at[step])
+
+
+def block_grads(features, w_first, w_second, items, meta, pairs):
+    nz, nx, nc = (lax.axis_size(a) for a in ROWS)
+    ny = lax.axis_size("grp")
     size, width = items.shape
     peers = nx * nc
+    plane, tiles = nz * peers, nz * nx
+    cap = max(2, 4 * size // plane)
+    share = width // ny
     vmem, dma = pltpu.VMEM, pltpu.SemaphoreType.DMA
     zh, xh = nz // 2, nx // 2
+    lane = ny * cap + 64
+    tower = (nc, ny, tiles, width // ny // tiles, width)
     return pl.pallas_call(
-        functools.partial(block_kernel, nz, nx, nc),
+        functools.partial(block_kernel, nz, nx, nc, ny),
         out_shape=(
-            jax.ShapeDtypeStruct((size, width), F32),
-            jax.ShapeDtypeStruct((2, width, width), F32),
+            jax.ShapeDtypeStruct((plane, ny // 2, cap, 2 * share), BF16),
+            jax.ShapeDtypeStruct((plane, 1, lane), jnp.int32),
+            jax.ShapeDtypeStruct(tower, F32),
         ),
-        in_specs=[pl.BlockSpec(memory_space=vmem)] * 5,
-        out_specs=[pl.BlockSpec(memory_space=vmem)] * 2,
+        in_specs=[pl.BlockSpec(memory_space=vmem)] * 6,
+        out_specs=[pl.BlockSpec(memory_space=vmem)] * 3,
         scratch_shapes=[
             vmem((peers * size, width), BF16),
             vmem((nz, size, width), BF16),
@@ -317,120 +502,88 @@
             dma((2, 2, zh)), dma((2, 2, zh)),
             dma((nx,)), dma((nx,)),
             dma((2, 2, xh)), dma((2, 2, xh)),
+            vmem((ny, 2, size), F32),
+            vmem((ny, 1, size), jnp.int32),
+            vmem((plane, 1, lane), jnp.int32),
+            vmem((ny, size // 2, 2 * share), BF16),
+            vmem((ny, size // 2, 2 * share), BF16),
+            vmem((plane, ny // 2, cap, 2 * share), BF16),
+            vmem((2, width, width), F32),
+            vmem((width, width), F32),
+            vmem((ny, width // ny, width), F32),
+            vmem((ny - 1, width // ny, width), F32),
+            vmem(tower[2:], F32),
+            vmem(tower[2:], F32),
+            dma((ny,)), dma((ny,)),
+            dma((plane,)), dma((plane,)),
+            dma((ny,)), dma((ny,)),
+            dma((plane,)), dma((plane,)),
+            dma, dma,
+            dma((ny,)), dma((ny,)),
+            dma((tiles,)), dma((tiles,)),
+            dma((tiles,)), dma((tiles,)),
+            dma((ny,)), dma((ny,)),
+            dma, dma,
         ],
         compiler_params=pltpu.CompilerParams(
             collective_id=0, has_side_effects=True, vmem_limit_bytes=60 * 2**20
         ),
         cost_estimate=pl.CostEstimate(flops=7 * 10**9, bytes_accessed=2**20, transcendentals=2**22),
         name="block_grads",
-    )(features, w_first, w_second, items, meta)
-
-
-def cut_along(value, dim, count):
-    before, after = (value.shape[:dim], value.shape[dim + 1 :])
-    return jnp.moveaxis(value.reshape(*before, count, -1, *after), dim, 0)
-
-
-def sum_at_owner(value, axis, dim):
-    count = lax.axis_size(axis)
-    tiles = lax.all_to_all(cut_along(value, dim, count), axis, 0, 0, tiled=True)
-    return jnp.sum(tiles, axis=0)
-
-
-def summed_rows(value, axes, dim):
-    far, near = axes
-    tiles = cut_along(value, dim, lax.axis_size(far))
-    nearer = sum_at_owner(tiles, near, dim + 1)
-    arrived = lax.all_to_all(nearer, far, split_axis=0, concat_axis=0, tiled=True)
-    return arrived.sum(axis=0)
-
-
-def padded_to(lines, count):
-    spare = -lines.shape[0] % count
-    if not spare:
-        return lines
-    return jnp.concatenate([lines, jnp.zeros((spare, *lines.shape[1:]), lines.dtype)])
-
-
-def sent_to_all(value, axis):
-    count = lax.axis_size(axis)
-    return lax.all_to_all(
-        jnp.broadcast_to(value[None], (count, *value.shape)), axis, 0, 0, tiled=True
-    )
-
-
-def joined_along(tiles, dim):
-    shape = list(tiles.shape[1:])
-    shape[dim] *= tiles.shape[0]
-    return jnp.moveaxis(tiles, 0, dim).reshape(shape)
-
-
-def gather_axes(value, axes, dim):
-    far, near = axes
-    tiles = sent_to_all(sent_to_all(value, far), near)
-    return joined_along(tiles.swapaxes(0, 1).reshape(-1, *value.shape), dim)
-
-
-def total_of(value, axes):
-    own = summed_rows(padded_to(value, lax.axis_size(axes[0]) * lax.axis_size(axes[1])), axes, 0)
-    whole = gather_axes(own, axes, 0)
-    return whole[: len(value)].reshape(value.shape)
-
-
-def in_one(arrays, axis):
-    flat, at, done = (jnp.concatenate([a.reshape(-1) for a in arrays]), 0, [])
-    total = total_of(flat, axis)
-    for a in arrays:
-        done.append(total[at : at + a.size].reshape(a.shape))
-        at += a.size
-    return tuple(done)
-
-
-def one_exchange(value, axis, axes, splits, concats):
-    sizes = [lax.axis_size(a) for a in axes]
-    tiles = cut_along(value, splits[0], sizes[0])
-    tiles = jnp.moveaxis(cut_along(tiles, splits[1] + 1, sizes[1]), 0, 1)
-    inside = tiles.shape[2:]
-    tiles = tiles.reshape(-1, *inside)
-    tiles = lax.all_to_all(tiles, axis, split_axis=0, concat_axis=0, tiled=True)
-    tiles = joined_along(tiles.reshape(*sizes, *inside), concats[0] + 1)
-    return joined_along(tiles, concats[1])
+    )(features, w_first, w_second, items, meta, pairs)
+
+
+def table_kernel(ids_ref, got_ref, out_ref, lines, *tables):
+    sources, pairs, cap, lanes = got_ref.shape
+    share = lanes // 2
+    count = out_ref.shape[0]
+    lines[...] = got_ref[...].astype(F32).reshape(lines.shape)
+    for table in tables:
+        table[...] = jnp.zeros_like(table)
+
+    @pl.loop(0, sources)
+    def _(source):
+        @pl.loop(0, ids_ref[source, 2 * pairs * cap])
+        def _(slot):
+            for pair in range(pairs):
+                line = lines[pl.ds((source * pairs + pair) * cap + slot, 1), :]
+                for side in (0, 1):
+                    g = 2 * pair + side
+                    at = pl.ds(ids_ref[source, g * cap + slot], 1)
+                    tables[g][at, :] += line
+
+    even = sum(t[:count, :] for t in tables[0::2])
+    odd = sum(t[:count, :] for t in tables[1::2])
+    out_ref[...] = even[:, :share] + odd[:, share:]
+
+
+def table_grads(ids, got):
+    sources, pairs, cap, lanes = got.shape
+    vmem = pltpu.VMEM
+    return pl.pallas_call(
+        table_kernel,
+        out_shape=jax.ShapeDtypeStruct((ITEMS_DEV, lanes // 2), F32),
+        in_specs=[pl.BlockSpec(memory_space=pltpu.SMEM), pl.BlockSpec(memory_space=vmem)],
+        out_specs=pl.BlockSpec(memory_space=vmem),
+        scratch_shapes=[vmem((sources * pairs * cap, lanes), F32)]
+        + [vmem((ITEMS_DEV + 8, lanes), F32)] * (2 * pairs),
+        compiler_params=pltpu.CompilerParams(vmem_limit_bytes=40 * 2**20),
+        name="table_grads",
+    )(ids, got)
 
 
 def body(
     user_features, w_first, w_second, item_embed, example_weight, positive, item_owner, item_row
 ):
-    own_items = item_embed[0]
-    owners = item_owner[0, :, 0]
-    item_rows = item_row[0]
-    my_users, feature_width = own_items.shape
-    peers = lax.axis_size(ROWS)
-    groups = lax.axis_size("grp")
-    capacity = max(2, 4 * my_users // peers)
-    member = (owners[:, None] == lax.broadcasted_iota(jnp.int32, (1, peers), 1)).astype(jnp.int32)
-    before = jnp.cumsum(member, axis=0) - member
-    slot_rank = jnp.sum(before * member, axis=1)
-    slots = owners * capacity + slot_rank
-    send_rows = (
-        jnp.full((peers * capacity,), -1.0, F32).at[slots].set(item_rows.astype(F32))
+    width = w_second.shape[1]
+    meta = jnp.stack([example_weight[0], positive[0].astype(F32)])
+    pairs = jnp.stack([item_owner[0, :, 0].astype(F32), item_row[0].astype(F32)])
+    got, ids, tower = block_grads(
+        user_features[0], w_first, w_second, item_embed[0], meta, pairs
     )
-    rows_wide = jnp.broadcast_to(send_rows.reshape(peers, capacity, 1), (peers, capacity, groups))
-    got_rows = one_exchange(rows_wide, ROWS_GRP, (ROWS, "grp"), (0, 2), (0, 1))
-    meta = jnp.stack([example_weight[0], positive[0].astype(F32)])
-    grad_item, tower = block_grads(user_features[0], w_first, w_second, own_items, meta)
-    send_grad = jnp.zeros((peers * capacity, feature_width), BF16).at[slots].set(grad_item.astype(BF16))
-    send_grad = send_grad.reshape(peers, capacity, feature_width)
-    got_grad = one_exchange(send_grad, ROWS_GRP, (ROWS, "grp"), (0, 2), (0, 1))
-    (summed,) = in_one((tower,), (("rows_0", "rows_1"), ("rows_2", "grp")))
-    share_width = feature_width // groups
-    table_rows = got_rows.reshape(-1).astype(jnp.int32)
-    table_rows = jnp.where(table_rows >= 0, table_rows, ITEMS_DEV)
-    grad_table = (
-        jnp.zeros((ITEMS_DEV, share_width), F32)
-        .at[table_rows]
-        .add(got_grad.reshape(-1, share_width).astype(F32), mode="drop")
-    )
-    return (summed[0].T, summed[1].T, grad_table)
+    grad_table = table_grads(ids.reshape(ids.shape[0], -1), got)
+    tower = tower.reshape(2, width, width)
+    return (tower[0].T, tower[1].T, grad_table)
 
 
 def solution(mesh):

time: 201 us -> 136 us (0.68)
  the two profiles are of different devices: /device:TPU:1 before, /device:TPU:71 now
where the time goes in v2:
time: 136 us; the launch traced here: 137 us
  Pallas kernels  129 us (95%)
  local copies, waits for them, and re-layouts  4.87 us (4%)
  other arithmetic  3.31 us (2%)
    pallas_call x1, Pallas kernels, block_grads(): pl.pallas_call(functools.partial(block_kernel, nz, nx, nc, ny), out_shape...  111 us
    pallas_call x1, Pallas kernels, table_grads(): pl.pallas_call(table_kernel, out_shape=jax.ShapeDtypeStruct((ITEMS_DEV, l...  17.6 us

profile of v2, /device:TPU:71, one launch (start us, length us, event | category | flops | bytes accessed | tf_op | source)
XLA Modules:
  0.0 137.4 jit_solution(10145589902818851699)
XLA Ops:
  0.6 0.7 convert_element_type.21
  1.3 0.7 convert_bitcast_fusion
  2.0 0.7 convert_element_type.24
  2.7 1.3 pad_maximum_fusion
  3.9 110.9 %block_grads.1 = (bf16[64,2,16,128]{3,2,1,0:T(8,128)(2,1)}, s32[64,1,128]{2,1,0:T(1,128)}, f32[2,4,32,2,256]{4,3,2,1,0:T(2,128)}) custom-call(bf16[256,256]{1,0:T(8,128)(2,1)} %bitcast.10, bf16[256,256]{1,0:T(8,128)(2,1)} %w1_ref.1, bf16[256,256]{1,0:T(8,128)(2,1)} %w2_ref.1, bf16[256,256]{1,0:T(8,128)(2,1)} %bitcast.11, ...), custom_call_target="tpu_custom_call" | custom-call | flops 7000000000 | bytes 1048576 | tf_op jit(solution)/shard_map/block_grads/pallas_call | solution.py:470
  114.8 0.0 copy-start
  114.8 0.0 copy-start.1
  114.8 1.3 fusion
  116.1 0.2 squeeze.18
  116.3 0.8 copy.12
  117.1 0.2 squeeze.17
  117.3 0.8 copy.11
  118.2 0.0 copy-done
  118.2 0.0 copy-done.1
  118.2 17.6 %table_grads.1 = f32[4096,64]{1,0:T(8,128)S(1)} custom-call(s32[64,128]{1,0:T(8,128)S(1)} %bitcast.7, bf16[64,2,16,128]{3,2,1,0:T(8,128)(2,1)S(1)} %copy-done), custom_call_target="tpu_custom_call" | custom-call | tf_op jit(solution)/shard_map/table_grads/pallas_call | solution.py:563
  135.8 1.6 %copy.13 = f32[4096,64]{0,1:T(8,128)} copy(f32[4096,64]{1,0:T(8,128)S(1)} %table_grads.1) | data formatting | bytes 2097152
Async XLA Ops:
  114.8 3.3 %copy-start = (bf16[64,2,16,128]{3,2,1,0:T(8,128)(2,1)S(1)}, bf16[64,2,16,128]{3,2,1,0:T(8,128)(2,1)}, u32[]{:S(2)}) copy-start(bf16[64,2,16,128]{3,2,1,0:T(8,128)(2,1)} %get-tuple-element.8.got_ref) | copy-start | bytes 1572868
  114.8 3.3 %copy-start.1 = (s32[64,1,128]{2,1,0:T(1,128)S(1)}, s32[64,1,128]{2,1,0:T(1,128)}, u32[]{:S(2)}) copy-start(s32[64,1,128]{2,1,0:T(1,128)} %get-tuple-element.7) | copy-start | bytes 98308

commit v3 on v2

--- a/solution.py
+++ b/solution.py
@@ -23,7 +23,8 @@
 
 
 def block_kernel(
-    nz, nx, nc, ny, feat_ref, w1_ref, w2_ref, items_ref, meta_ref, pairs_ref, got_ref, ids_ref, tower_ref,
+    nz, nx, nc, ny, feat_ref, w1_ref, w2_ref, items_ref, weight_ref, target_ref, owner_ref, row_ref,
+    got_ref, ids_ref, tower_ref,
     users, items_all, items_turned, meta_all, peaks, sums, lses, scale, probs, ds,
     gi_part, gu_part, gu_pair, z_land, x_land, pre_keep, hid_keep,
     z_send, z_recv, x_send, x_recv, p_send, p_recv, m_send, m_recv, l_send, l_recv,
@@ -117,15 +118,19 @@
     def block_rows(block):
         return pl.ds(pl.multiple_of(block * size, size), size)
 
-    pre = jnp.dot(feat_ref[...], w1_ref[...], preferred_element_type=F32)
-    hidden = (pre * jax.nn.sigmoid(pre)).astype(BF16)
-    hid_keep[...] = hidden
-    users[block_rows(me), :] = jnp.dot(hidden, w2_ref[...], preferred_element_type=F32).astype(BF16)
-    items_all[z] = items_ref[...]
-    meta_all[me] = meta_ref[...]
-
-    pairs_all[y] = pairs_ref[...]
-    pl.semaphore_wait(barrier, plane - 1 + ny - 1)
+    with jax.named_scope("tower"):
+        pre = jnp.dot(feat_ref[...], w1_ref[...], preferred_element_type=F32)
+        hidden = (pre * jax.nn.sigmoid(pre)).astype(BF16)
+        hid_keep[...] = hidden
+        users[block_rows(me), :] = jnp.dot(hidden, w2_ref[...], preferred_element_type=F32).astype(BF16)
+        items_all[z] = items_ref[...]
+        meta_all[me, 0:1, :] = weight_ref[...]
+        meta_all[me, 1:2, :] = target_ref[...].astype(F32)
+
+        pairs_all[y, 0:1, :] = owner_ref[...].astype(F32)
+        pairs_all[y, 1:2, :] = row_ref[...].astype(F32)
+    with jax.named_scope("barrier"):
+        pl.semaphore_wait(barrier, plane - 1 + ny - 1)
 
     def z_forward(r):
         for way, sign in enumerate(signs):
@@ -162,16 +167,17 @@
                     place = users.at[rows_of(x_at(-sign * r) * nc + 1 - c, half)]
                     arrived(place, p_recv.at[way, half, r])
 
-    x_forward(0)
-    z_forward(0)
-    for step in range(1, peers):
-        send(meta_all.at[me], meta_all.at[me], m_send.at[step], m_recv.at[step], peer(step))
-
-    for step in range(1, ny):
-        send(pairs_all.at[y], pairs_all.at[y], i_send.at[step], i_recv.at[step],
-             {"grp": y_at(step)})
-
-    pre_keep[...] = pre.T
+    with jax.named_scope("start"):
+        x_forward(0)
+        z_forward(0)
+        for step in range(1, peers):
+            send(meta_all.at[me], meta_all.at[me], m_send.at[step], m_recv.at[step], peer(step))
+
+        for step in range(1, ny):
+            send(pairs_all.at[y], pairs_all.at[y], i_send.at[step], i_recv.at[step],
+                 {"grp": y_at(step)})
+
+        pre_keep[...] = pre.T
 
     cap = got_ref.shape[2]
     share = got_ref.shape[3] // 2
@@ -206,71 +212,73 @@
         named = jnp.concatenate(pieces, axis=1).astype(jnp.int32)
         ids_out[...] = named.reshape(ids_out.shape)
 
-    for r in range(1, nx // 2 + 1):
-        x_forward(r)
-        if r == 1:
-            z_forward(1)
-            for step in range(1, ny):
-                arrived(pairs_all.at[y_at(-step)], i_recv.at[step])
-            name_slots()
-    from_partner()
+    with jax.named_scope("users"):
+        for r in range(1, nx // 2 + 1):
+            x_forward(r)
+            if r == 1:
+                z_forward(1)
+                for step in range(1, ny):
+                    arrived(pairs_all.at[y_at(-step)], i_recv.at[step])
+                name_slots()
+        from_partner()
 
     def first_pass(chunk):
         own = items_all[chunk]
         items_turned[:, block_rows(chunk)] = own.T
 
-        @pl.loop(0, peers)
-        def _(k):
-            s = contract(items_all[chunk], users[block_rows(k), :], (1, 1))
+        for k in range(peers):
+            s = contract(own, users[k * size : (k + 1) * size, :], (1, 1))
             top = jnp.max(s, axis=0, keepdims=True)
             p = jnp.exp(s - top)
             probs[chunk * peers + k] = p
-            peaks[chunk, pl.ds(k, 1), :] = top
-            sums[chunk, pl.ds(k, 1), :] = jnp.sum(p, axis=0, keepdims=True)
-
-    first_pass(z)
-
-    @pl.loop(1, plane)
-    def _(step):
-        where, there = far(step)
-        send_plainly(ids_out.at[there], ids_ref.at[here], n_send.at[step], n_recv.at[step], where)
-
-    ids_ref[here] = ids_out[here]
-    for r in range(1, nz // 2 + 1):
-        if r > 1:
-            z_forward(r)
-        if r < nz // 2:
-            first_pass(z_at(r))
-            first_pass(z_at(-r))
-        else:
-            first_pass(z_at(r))
-
-    tops = peaks[...]
-    top = jnp.max(tops, axis=0)
-    lses[me] = top + jnp.log(jnp.sum(sums[...] * jnp.exp(tops - top[None]), axis=0))
-    for step in range(1, peers):
-        send(lses.at[me], lses.at[me], l_send.at[step], l_recv.at[step], peer(step))
-    for step in range(1, peers):
-        arrived(meta_all.at[from_peer(step)], m_recv.at[step])
-    for step in range(1, peers):
-        arrived(lses.at[from_peer(step)], l_recv.at[step])
-    parts = lses[...]
-    top = jnp.max(parts, axis=0)
-    total = top + jnp.log(jnp.sum(jnp.exp(parts - top[None]), axis=0))
-    scale[...] = jnp.exp(tops - total[None])
+            peaks[chunk, k : k + 1, :] = top
+            sums[chunk, k : k + 1, :] = jnp.sum(p, axis=0, keepdims=True)
+
+    with jax.named_scope("first"):
+        first_pass(z)
+
+        @pl.loop(1, plane)
+        def _(step):
+            where, there = far(step)
+            send_plainly(ids_out.at[there], ids_ref.at[here], n_send.at[step], n_recv.at[step], where)
+
+        ids_ref[here] = ids_out[here]
+        for r in range(1, nz // 2 + 1):
+            if r > 1:
+                z_forward(r)
+            if r < nz // 2:
+                @pl.loop(0, 2)
+                def _(side):
+                    first_pass(lax.rem(z + nz + r - 2 * r * side, nz))
+            else:
+                first_pass(z_at(r))
+
+    with jax.named_scope("lse"):
+        tops = peaks[...]
+        top = jnp.max(tops, axis=0)
+        lses[me] = top + jnp.log(jnp.sum(sums[...] * jnp.exp(tops - top[None]), axis=0))
+        for step in range(1, peers):
+            send(lses.at[me], lses.at[me], l_send.at[step], l_recv.at[step], peer(step))
+        for step in range(1, peers):
+            arrived(meta_all.at[from_peer(step)], m_recv.at[step])
+        for step in range(1, peers):
+            arrived(lses.at[from_peer(step)], l_recv.at[step])
+        parts = lses[...]
+        top = jnp.max(parts, axis=0)
+        total = top + jnp.log(jnp.sum(jnp.exp(parts - top[None]), axis=0))
+        scale[...] = jnp.exp(tops - total[None])
 
     lines = lax.broadcasted_iota(jnp.int32, (size, size), 0)
 
     def second_pass(chunk):
         first = ((chunk * nx + x) * nc + c) * size
 
-        @pl.loop(0, peers)
-        def _(k):
+        for k in range(peers):
             weight = meta_all[k, 0:1, :]
             target = meta_all[k, 1:2, :].astype(jnp.int32) - first
-            t = probs[chunk * peers + k] * (scale[chunk, pl.ds(k, 1), :] * weight)
+            t = probs[chunk * peers + k] * (scale[chunk, k : k + 1, :] * weight)
             t = jnp.where(lines == target, t - weight, t)
-            ds[block_rows(chunk), block_rows(k)] = t.astype(BF16)
+            ds[block_rows(chunk), k * size : (k + 1) * size] = t.astype(BF16)
 
         gi_part[chunk] = jnp.dot(ds[block_rows(chunk), :], users[...], preferred_element_type=F32)
 
@@ -290,30 +298,34 @@
                 send(src, z_land.at[way, half, r], zr_send.at[way, half, r],
                      zr_recv.at[way, half, r], {"rows_0": z_at(sign)})
 
-    second_pass(z_at(nz // 2))
-    z_reduce(0, ((0, 0), (1, 1)))
-    second_pass(z_at(nz // 2 - 1))
-    z_reduce(0, ((0, 1),))
-    second_pass(z_at(1 - nz // 2))
-    z_reduce(0, ((1, 0),))
-    for r in range(nz // 2 - 2, 0, -1):
-        second_pass(z_at(r))
-        second_pass(z_at(-r))
-    second_pass(z)
+    with jax.named_scope("second"):
+        second_pass(z_at(nz // 2))
+        z_reduce(0, ((0, 0), (1, 1)))
+        second_pass(z_at(nz // 2 - 1))
+        z_reduce(0, ((0, 1),))
+        second_pass(z_at(1 - nz // 2))
+        z_reduce(0, ((1, 0),))
+        left = 2 * (nz // 2 - 2) + 1
+
+        @pl.loop(0, left)
+        def _(i):
+            second_pass(lax.rem(z + nz + ((left - i) // 2) * (1 - 2 * lax.rem(i, 2)), nz))
 
     def user_pass(k):
         gu_part[k] = jnp.dot(items_turned[...], ds[:, block_rows(k)], preferred_element_type=F32)
 
-    z_reduce(1)
-    for step in range(nx):
-        k = x_at(step) * nc + 1 - c
-        user_pass(k)
-        send(gu_part.at[k], gu_pair.at[x_at(step)], d_send.at[step], d_recv.at[step], partner)
-    for step in range(nx):
-        user_pass(x_at(step) * nc + c)
-    for step in range(nx):
-        arrived(gu_pair.at[x_at(step)], d_recv.at[step])
-        gu_pair[x_at(step)] += gu_part[x_at(step) * nc + c]
+    with jax.named_scope("zr1"):
+        z_reduce(1)
+    with jax.named_scope("userpass"):
+        for step in range(nx):
+            k = x_at(step) * nc + 1 - c
+            user_pass(k)
+            send(gu_part.at[k], gu_pair.at[x_at(step)], d_send.at[step], d_recv.at[step], partner)
+        for step in range(nx):
+            user_pass(x_at(step) * nc + c)
+        for step in range(nx):
+            arrived(gu_pair.at[x_at(step)], d_recv.at[step])
+            gu_pair[x_at(step)] += gu_part[x_at(step) * nc + c]
 
     def x_reduce(r):
         for way, sign in enumerate(signs):
@@ -331,131 +343,142 @@
                     send(src, x_land.at[way, half, r], xr_send.at[way, half, r],
                          xr_recv.at[way, half, r], {"rows_1": x_at(sign)})
 
-    x_reduce(0)
-    for r in range(1, nx // 2 + 1):
-        if r + 1 <= nz // 2:
-            z_reduce(r + 1)
-        x_reduce(r)
-
-    def collected(own, land, n):
-        pieces = []
-        for half in (0, 1):
-            got = own[half * half_size : (half + 1) * half_size]
-            for way in (0, 1):
-                length = chain_length(n, way, half)
-                if length:
-                    got = got + land[way, half, length - 1]
-            pieces.append(got)
-        return jnp.concatenate(pieces, axis=0)
-
-    gu = collected(gu_pair[x], x_land, nx).astype(BF16)
-    pre = pre_keep[...]
-    gate = jax.nn.sigmoid(pre)
-    back = jnp.dot(w2_ref[...], gu, preferred_element_type=F32)
-    grad_pre = (back * gate * (1.0 + pre * (1.0 - gate))).astype(BF16)
-    df_keep[0] = jnp.dot(grad_pre, feat_ref[...], preferred_element_type=F32)
-    df_keep[1] = jnp.dot(gu, hid_keep[...], preferred_element_type=F32)
-
-    send(df_keep.at[1 - c], df_pair, ac_send, ac_recv, partner)
-    arrived(df_pair, ac_recv)
-    y_part[...] = (df_keep[c] + df_pair[...]).reshape(y_part.shape)
-    for step in range(1, ny):
-        send(y_part.at[y_at(step)], y_land.at[step - 1], ay_send.at[step], ay_recv.at[step],
-             {"grp": y_at(step)})
-
-    for r in range(nx // 2 + 2, nz // 2 + 1):
-        z_reduce(r)
-    gi = collected(gi_part[z], z_land, nz).astype(BF16)
-
-    for to in range(ny):
-        cols = slice(to * share, (to + 1) * share)
-        share_out[to] = jnp.concatenate([gi[:half_size, cols], gi[half_size:, cols]], axis=1)
-    for step in range(1, ny):
-        send(share_out.at[y_at(step)], share_in.at[y], s_send.at[step], s_recv.at[step],
-             {"grp": y_at(step)})
-    share_in[y] = share_out[y]
-
-    whole = y_part[y]
-    for step in range(1, ny):
-        arrived(y_land.at[step - 1], ay_recv.at[step])
-        whole = whole + y_land[step - 1]
-    p_part[...] = whole.reshape(p_part.shape)
-
-    @pl.loop(1, tiles)
-    def _(step):
-        where, there = far_tile(step)
-        send_plainly(p_part.at[there], p_land.at[step], ap_send.at[step], ap_recv.at[step], where)
-
-    for step in range(1, ny):
-        arrived(share_in.at[y_at(-step)], s_recv.at[step])
-    slot_lines = lax.broadcasted_iota(jnp.int32, (plane * cap, size), 0)
-    for pair in range(ny // 2):
-        sides = []
-        for g in (2 * pair, 2 * pair + 1):
-            chosen = (slot_lines == slots_keep[g]).astype(BF16)
-            packed = share_in[g]
-            data = jnp.concatenate([packed[:, :share], packed[:, share:]], axis=0)
-            sides.append(jnp.dot(chosen, data, preferred_element_type=F32))
-        both = jnp.concatenate(sides, axis=1).astype(BF16)
-        slotted[:, pair] = both.reshape(plane, cap, 2 * share)
-    got_ref[here] = slotted[here]
-
-    def exchange(first, last):
-        @pl.loop(first, last)
-        def _(step):
-            where, there = far(step)
-            send_plainly(slotted.at[there], got_ref.at[here], e_send.at[step], e_recv.at[step],
-                         where)
-
-    exchange(1, plane // 2)
-    p_land[0] = p_part[tile]
-
-    @pl.loop(1, tiles)
-    def _(step):
-        arrived(p_land.at[step], ap_recv.at[step])
-
-    own = tower_ref.at[c, y, tile]
-    own[...] = jnp.sum(p_land[...], axis=0)
-
-    @pl.loop(1, tiles)
-    def _(step):
-        where, _ = far_tile(step)
-        send_plainly(own, own, gp_send.at[step], gp_recv.at[step], where)
-
-    exchange(plane // 2, plane)
-
-    @pl.loop(1, tiles)
-    def _(step):
-        arrived(tower_ref.at[c, y, from_far_tile(step)], gp_recv.at[step])
-
-    for step in range(1, ny):
-        send(tower_ref.at[c, y], tower_ref.at[c, y], gy_send.at[step], gy_recv.at[step],
-             {"grp": y_at(step)})
-    for step in range(1, ny):
-        arrived(tower_ref.at[c, y_at(-step)], gy_recv.at[step])
-    send(tower_ref.at[c], tower_ref.at[c], gc_send, gc_recv, partner)
-
-    @pl.loop(1, plane)
-    def _(step):
-        arrived(ids_ref.at[from_far(step)], n_recv.at[step])
-        arrived(got_ref.at[from_far(step)], e_recv.at[step])
-
-    arrived(tower_ref.at[1 - c], gc_recv)
-    for copy in pending:
-        copy.wait_send()
-
-    @pl.loop(1, plane)
-    def _(step):
-        arrived(ids_out.at[0], n_send.at[step])
-        arrived(slotted.at[0], e_send.at[step])
-
-    @pl.loop(1, tiles)
-    def _(step):
-        arrived(p_part.at[0], ap_send.at[step])
-        arrived(p_part.at[0], gp_send.at[step])
-
-
-def block_grads(features, w_first, w_second, items, meta, pairs):
+    with jax.named_scope("reduce"):
+        x_reduce(0)
+        for r in range(1, nx // 2 + 1):
+            if r + 1 <= nz // 2:
+                z_reduce(r + 1)
+            x_reduce(r)
+
+        def collected(own, land, n):
+            pieces = []
+            for half in (0, 1):
+                got = own[half * half_size : (half + 1) * half_size]
+                for way in (0, 1):
+                    length = chain_length(n, way, half)
+                    if length:
+                        got = got + land[way, half, length - 1]
+                pieces.append(got)
+            return jnp.concatenate(pieces, axis=0)
+
+    with jax.named_scope("towerback"):
+        gu = collected(gu_pair[x], x_land, nx).astype(BF16)
+        pre = pre_keep[...]
+        gate = jax.nn.sigmoid(pre)
+        back = jnp.dot(w2_ref[...], gu, preferred_element_type=F32)
+        grad_pre = (back * gate * (1.0 + pre * (1.0 - gate))).astype(BF16)
+        df_keep[0] = jnp.dot(grad_pre, feat_ref[...], preferred_element_type=F32)
+        df_keep[1] = jnp.dot(gu, hid_keep[...], preferred_element_type=F32)
+
+    with jax.named_scope("zrlast"):
+        send(df_keep.at[1 - c], df_pair, ac_send, ac_recv, partner)
+        for r in range(nx // 2 + 2, nz // 2 + 1):
+            z_reduce(r)
+        gi = collected(gi_part[z], z_land, nz).astype(BF16)
+    with jax.named_scope("shares"):
+        for to in range(ny):
+            cols = slice(to * share, (to + 1) * share)
+            share_out[to] = jnp.concatenate([gi[:half_size, cols], gi[half_size:, cols]], axis=1)
+        for step in range(1, ny):
+            send(share_out.at[y_at(step)], share_in.at[y], s_send.at[step], s_recv.at[step],
+                 {"grp": y_at(step)})
+        share_in[y] = share_out[y]
+    with jax.named_scope("acy"):
+        arrived(df_pair, ac_recv)
+        y_part[...] = (df_keep[c] + df_pair[...]).reshape(y_part.shape)
+        for step in range(1, ny):
+            send(y_part.at[y_at(step)], y_land.at[step - 1], ay_send.at[step], ay_recv.at[step],
+                 {"grp": y_at(step)})
+    with jax.named_scope("sharewait"):
+        for step in range(1, ny):
+            arrived(share_in.at[y_at(-step)], s_recv.at[step])
+    with jax.named_scope("slots"):
+        slot_lines = lax.broadcasted_iota(jnp.int32, (plane * cap, size), 0)
+        for pair in range(ny // 2):
+            sides = []
+            for g in (2 * pair, 2 * pair + 1):
+                chosen = (slot_lines == slots_keep[g]).astype(BF16)
+                packed = share_in[g]
+                data = jnp.concatenate([packed[:, :share], packed[:, share:]], axis=0)
+                sides.append(jnp.dot(chosen, data, preferred_element_type=F32))
+            both = jnp.concatenate(sides, axis=1).astype(BF16)
+            slotted[:, pair] = both.reshape(plane, cap, 2 * share)
+
+        def exchange(first, last):
+            @pl.loop(first, last)
+            def _(step):
+                where, there = far(step)
+                send_plainly(slotted.at[there], got_ref.at[here], e_send.at[step], e_recv.at[step],
+                             where)
+
+        exchange(1, plane // 4)
+        got_ref[here] = slotted[here]
+    with jax.named_scope("ysum"):
+        whole = y_part[y]
+        for step in range(1, ny):
+            arrived(y_land.at[step - 1], ay_recv.at[step])
+            whole = whole + y_land[step - 1]
+        p_part[...] = whole.reshape(p_part.shape)
+
+        @pl.loop(1, tiles)
+        def _(step):
+            where, there = far_tile(step)
+            send_plainly(p_part.at[there], p_land.at[step], ap_send.at[step], ap_recv.at[step], where)
+
+        exchange(plane // 4, plane // 2)
+        p_land[0] = p_part[tile]
+    with jax.named_scope("planesum"):
+        @pl.loop(1, tiles)
+        def _(step):
+            arrived(p_land.at[step], ap_recv.at[step])
+
+        own = tower_ref.at[c, y, tile]
+        own[...] = jnp.sum(p_land[...], axis=0)
+
+        @pl.loop(1, tiles)
+        def _(step):
+            where, _ = far_tile(step)
+            send_plainly(own, own, gp_send.at[step], gp_recv.at[step], where)
+
+        exchange(plane // 2, plane)
+    with jax.named_scope("planeback"):
+
+        @pl.loop(1, tiles)
+        def _(step):
+            arrived(tower_ref.at[c, y, from_far_tile(step)], gp_recv.at[step])
+
+    with jax.named_scope("yback"):
+        for step in range(1, ny):
+            send(tower_ref.at[c, y], tower_ref.at[c, y], gy_send.at[step], gy_recv.at[step],
+                 {"grp": y_at(step)})
+        for step in range(1, ny):
+            arrived(tower_ref.at[c, y_at(-step)], gy_recv.at[step])
+        send(tower_ref.at[c], tower_ref.at[c], gc_send, gc_recv, partner)
+
+    with jax.named_scope("got"):
+        @pl.loop(1, plane)
+        def _(step):
+            arrived(ids_ref.at[from_far(step)], n_recv.at[step])
+            arrived(got_ref.at[from_far(step)], e_recv.at[step])
+
+    with jax.named_scope("cback"):
+        arrived(tower_ref.at[1 - c], gc_recv)
+    with jax.named_scope("sent"):
+        for copy in pending:
+            copy.wait_send()
+
+        @pl.loop(1, plane)
+        def _(step):
+            arrived(ids_out.at[0], n_send.at[step])
+            arrived(slotted.at[0], e_send.at[step])
+
+        @pl.loop(1, tiles)
+        def _(step):
+            arrived(p_part.at[0], ap_send.at[step])
+            arrived(p_part.at[0], gp_send.at[step])
+
+
+def block_grads(features, w_first, w_second, items, *columns):
     nz, nx, nc = (lax.axis_size(a) for a in ROWS)
     ny = lax.axis_size("grp")
     size, width = items.shape
@@ -474,7 +497,7 @@
             jax.ShapeDtypeStruct((plane, 1, lane), jnp.int32),
             jax.ShapeDtypeStruct(tower, F32),
         ),
-        in_specs=[pl.BlockSpec(memory_space=vmem)] * 6,
+        in_specs=[pl.BlockSpec(memory_space=vmem)] * 8,
         out_specs=[pl.BlockSpec(memory_space=vmem)] * 3,
         scratch_shapes=[
             vmem((peers * size, width), BF16),
@@ -530,60 +553,71 @@
         ),
         cost_estimate=pl.CostEstimate(flops=7 * 10**9, bytes_accessed=2**20, transcendentals=2**22),
         name="block_grads",
-    )(features, w_first, w_second, items, meta, pairs)
-
-
-def table_kernel(ids_ref, got_ref, out_ref, lines, *tables):
+    )(features, w_first, w_second, items, *columns)
+
+
+def table_kernel(ids_ref, got_ref, tower_ref, out_ref, first_ref, second_ref, lines, *tables):
     sources, pairs, cap, lanes = got_ref.shape
     share = lanes // 2
-    count = out_ref.shape[0]
+    width = first_ref.shape[0]
+    count = out_ref.shape[1]
+    step = 4
     lines[...] = got_ref[...].astype(F32).reshape(lines.shape)
     for table in tables:
         table[...] = jnp.zeros_like(table)
 
     @pl.loop(0, sources)
     def _(source):
-        @pl.loop(0, ids_ref[source, 2 * pairs * cap])
-        def _(slot):
-            for pair in range(pairs):
-                line = lines[pl.ds((source * pairs + pair) * cap + slot, 1), :]
-                for side in (0, 1):
-                    g = 2 * pair + side
-                    at = pl.ds(ids_ref[source, g * cap + slot], 1)
-                    tables[g][at, :] += line
-
-    even = sum(t[:count, :] for t in tables[0::2])
-    odd = sum(t[:count, :] for t in tables[1::2])
-    out_ref[...] = even[:, :share] + odd[:, share:]
-
-
-def table_grads(ids, got):
+        @pl.loop(0, (ids_ref[source, 2 * pairs * cap] + (step - 1)) // step)
+        def _(block):
+            for slot in range(step):
+                slot = block * step + slot
+                for pair in range(pairs):
+                    line = lines[pl.ds((source * pairs + pair) * cap + slot, 1), :]
+                    for side in (0, 1):
+                        g = 2 * pair + side
+                        at = pl.ds(ids_ref[source, g * cap + slot], 1)
+                        tables[g][at, :] += line
+
+    part = min(count, 512)
+    for at in range(0, count, part):
+        rows = slice(at, at + part)
+        even = sum(t[rows, :] for t in tables[0::2])
+        odd = sum(t[rows, :] for t in tables[1::2])
+        out_ref[:, rows] = even.T[:share, :] + odd.T[share:, :]
+    first_ref[...] = tower_ref[0].reshape(width, width).T
+    second_ref[...] = tower_ref[1].reshape(width, width).T
+
+
+def table_grads(ids, got, tower):
     sources, pairs, cap, lanes = got.shape
+    width = tower.shape[-1]
     vmem = pltpu.VMEM
     return pl.pallas_call(
         table_kernel,
-        out_shape=jax.ShapeDtypeStruct((ITEMS_DEV, lanes // 2), F32),
-        in_specs=[pl.BlockSpec(memory_space=pltpu.SMEM), pl.BlockSpec(memory_space=vmem)],
-        out_specs=pl.BlockSpec(memory_space=vmem),
+        out_shape=(
+            jax.ShapeDtypeStruct((lanes // 2, ITEMS_DEV), F32),
+            jax.ShapeDtypeStruct((width, width), F32),
+            jax.ShapeDtypeStruct((width, width), F32),
+        ),
+        in_specs=[pl.BlockSpec(memory_space=pltpu.SMEM)] + [pl.BlockSpec(memory_space=vmem)] * 2,
+        out_specs=[pl.BlockSpec(memory_space=vmem)] * 3,
         scratch_shapes=[vmem((sources * pairs * cap, lanes), F32)]
         + [vmem((ITEMS_DEV + 8, lanes), F32)] * (2 * pairs),
         compiler_params=pltpu.CompilerParams(vmem_limit_bytes=40 * 2**20),
         name="table_grads",
-    )(ids, got)
+    )(ids, got, tower)
 
 
 def body(
     user_features, w_first, w_second, item_embed, example_weight, positive, item_owner, item_row
 ):
-    width = w_second.shape[1]
-    meta = jnp.stack([example_weight[0], positive[0].astype(F32)])
-    pairs = jnp.stack([item_owner[0, :, 0].astype(F32), item_row[0].astype(F32)])
     got, ids, tower = block_grads(
-        user_features[0], w_first, w_second, item_embed[0], meta, pairs
+        user_features[0], w_first, w_second, item_embed[0],
+        example_weight, positive, item_owner.reshape(positive.shape), item_row,
     )
-    grad_table = table_grads(ids.reshape(ids.shape[0], -1), got)
-    tower = tower.reshape(2, width, width)
-    return (tower[0].T, tower[1].T, grad_table)
+    table, first, second = table_grads(ids.reshape(ids.shape[0], -1), got, tower)
+    return (first, second, table.T)
 
 
 def solution(mesh):

time: 136 us -> 122 us (0.90)
  the two profiles are of different devices: /device:TPU:71 before, /device:TPU:1 now
where the time goes in v3:
time: 122 us; the launch traced here: 124 us
  Pallas kernels  120 us (98%)
  local copies, waits for them, and re-layouts  2.83 us (2%)
    pallas_call x1, Pallas kernels, block_grads(): pl.pallas_call(functools.partial(block_kernel, nz, nx, nc, ny), out_shape...  105 us
    pallas_call x1, Pallas kernels, table_grads(): pl.pallas_call(table_kernel, out_shape=(jax.ShapeDtypeStruct((lanes // 2,...  15.4 us
    unnamed x6, local copies, waits for them, and re-layouts  2.83 us

profile of v3, /device:TPU:1, one launch (start us, length us, event | category | flops | bytes accessed | tf_op | source)
XLA Modules:
  0.0 123.7 jit_solution(12381788659235459941)
XLA Ops:
  0.6 104.9 %block_grads.1 = (bf16[64,2,16,128]{3,2,1,0:T(8,128)(2,1)}, s32[64,1,128]{2,1,0:T(1,128)}, f32[2,4,32,2,256]{4,3,2,1,0:T(2,128)}) custom-call(bf16[256,256]{1,0:T(8,128)(2,1)} %bitcast.7, bf16[256,256]{1,0:T(8,128)(2,1)} %w1_ref.1, bf16[256,256]{1,0:T(8,128)(2,1)} %w2_ref.1, bf16[256,256]{1,0:T(8,128)(2,1)} %bitcast.8, f32[1,256]{1,0:T(1,128)} %weight_ref.1, ...), custom_call_target="tpu_custom_call" | custom-call | flops 7000000000 | bytes 1048576 | tf_op jit(solution)/shard_map/block_grads/pallas_call | solution.py:493
  105.5 0.0 copy-start
  105.5 1.0 copy-done
  106.5 0.0 copy-start.1
  106.5 1.0 copy-done.1
  107.6 0.0 copy-start.2
  107.6 0.8 copy-done.2
  108.3 15.4 %table_grads.1 = (f32[64,4096]{1,0:T(8,128)}, f32[256,256]{1,0:T(8,128)}, f32[256,256]{1,0:T(8,128)}) custom-call(s32[64,128]{1,0:T(8,128)S(1)} %bitcast.5, bf16[64,2,16,128]{3,2,1,0:T(8,128)(2,1)S(1)} %copy-done, f32[2,4,32,2,256]{4,3,2,1,0:T(2,128)S(1)} %copy-done.1), custom_call_target="tpu_custom_call" | custom-call | tf_op jit(solution)/shard_map/table_grads/pallas_call | solution.py:596
Async XLA Ops:
  105.5 1.0 copy-start
  106.5 1.0 copy-start.1
  107.6 0.8 copy-start.2

commit v4 on v3

--- a/solution.py
+++ b/solution.py
@@ -8,6 +8,7 @@
 from jax.sharding import PartitionSpec as P
 
 ITEMS_DEV = 4096
+HIGH = 256
 ROWS = ("rows_0", "rows_1", "rows_2")
 MESH = pl.DeviceIdType.MESH
 F32 = jnp.float32
@@ -24,7 +25,7 @@
 
 def block_kernel(
     nz, nx, nc, ny, feat_ref, w1_ref, w2_ref, items_ref, weight_ref, target_ref, owner_ref, row_ref,
-    got_ref, ids_ref, tower_ref,
+    table_ref, first_ref, second_ref,
     users, items_all, items_turned, meta_all, peaks, sums, lses, scale, probs, ds,
     gi_part, gu_part, gu_pair, z_land, x_land, pre_keep, hid_keep,
     z_send, z_recv, x_send, x_recv, p_send, p_recv, m_send, m_recv, l_send, l_recv,
@@ -34,6 +35,7 @@
     i_send, i_recv, n_send, n_recv, s_send, s_recv, e_send, e_recv,
     ac_send, ac_recv, ay_send, ay_recv, ap_send, ap_recv,
     gp_send, gp_recv, gy_send, gy_recv, gc_send, gc_recv,
+    landed, ids_land, tower, low_all, high_all, spread_left, spread_right, acc,
 ):
     z, x, c = lax.axis_index("rows_0"), lax.axis_index("rows_1"), lax.axis_index("rows_2")
     y = lax.axis_index("grp")
@@ -42,6 +44,7 @@
     peers = nx * nc
     me = x * nc + c
     signs = (1, -1)
+    early, late = ((0, 0), (1, 1)), ((0, 1), (1, 0))
 
     def z_at(step):
         return lax.rem(z + step + nz, nz)
@@ -132,33 +135,33 @@
     with jax.named_scope("barrier"):
         pl.semaphore_wait(barrier, plane - 1 + ny - 1)
 
-    def z_forward(r):
-        for way, sign in enumerate(signs):
-            for half in (0, 1):
-                length = chain_length(nz, way, half)
-                rows = pl.ds(half * half_size, half_size)
-                if 1 <= r <= length:
-                    arrived(items_all.at[z_at(-sign * r), rows], z_recv.at[way, half, r - 1])
-                if r < length:
-                    block = z_at(-sign * r)
-                    src = items_ref.at[rows] if r == 0 else items_all.at[block, rows]
-                    send(src, items_all.at[block, rows], z_send.at[way, half, r],
-                         z_recv.at[way, half, r], {"rows_0": z_at(sign)})
-
-    def x_forward(r):
-        for way, sign in enumerate(signs):
-            for half in (0, 1):
-                length = chain_length(nx, way, half)
-                place = users.at[rows_of(x_at(-sign * r) * nc + c, half)]
-                if 1 <= r <= length:
-                    arrived(place, x_recv.at[way, half, r - 1])
-                if r < length:
-                    send(place, place, x_send.at[way, half, r], x_recv.at[way, half, r],
-                         {"rows_1": x_at(sign)})
-                if 1 <= r <= length:
-                    send(place, place, p_send.at[way, half, r], p_recv.at[way, half, r], partner)
-                if r == 0 and way == 0:
-                    send(place, place, p_send.at[way, half, 0], p_recv.at[way, half, 0], partner)
+    def z_forward(r, parts_of):
+        for way, half in parts_of:
+            sign = signs[way]
+            length = chain_length(nz, way, half)
+            rows = pl.ds(half * half_size, half_size)
+            block = z_at(-sign * r)
+            if 1 <= r <= length:
+                arrived(items_all.at[block, rows], z_recv.at[way, half, r - 1])
+            if r < length:
+                src = items_ref.at[rows] if r == 0 else items_all.at[block, rows]
+                send(src, items_all.at[block, rows], z_send.at[way, half, r],
+                     z_recv.at[way, half, r], {"rows_0": z_at(sign)})
+
+    def x_forward(r, parts_of):
+        for way, half in parts_of:
+            sign = signs[way]
+            length = chain_length(nx, way, half)
+            place = users.at[rows_of(x_at(-sign * r) * nc + c, half)]
+            if 1 <= r <= length:
+                arrived(place, x_recv.at[way, half, r - 1])
+            if r < length:
+                send(place, place, x_send.at[way, half, r], x_recv.at[way, half, r],
+                     {"rows_1": x_at(sign)})
+            if 1 <= r <= length:
+                send(place, place, p_send.at[way, half, r], p_recv.at[way, half, r], partner)
+            if r == 0 and way == 0:
+                send(place, place, p_send.at[way, half, 0], p_recv.at[way, half, 0], partner)
 
     def from_partner():
         for way, sign in enumerate(signs):
@@ -168,8 +171,9 @@
                     arrived(place, p_recv.at[way, half, r])
 
     with jax.named_scope("start"):
-        x_forward(0)
-        z_forward(0)
+        for parts in (early, late):
+            x_forward(0, parts)
+            z_forward(0, parts)
         for step in range(1, peers):
             send(meta_all.at[me], meta_all.at[me], m_send.at[step], m_recv.at[step], peer(step))
 
@@ -179,8 +183,8 @@
 
         pre_keep[...] = pre.T
 
-    cap = got_ref.shape[2]
-    share = got_ref.shape[3] // 2
+    cap = landed.shape[2]
+    share = landed.shape[3] // 2
 
     def name_slots():
         earlier = (
@@ -189,7 +193,7 @@
         ).astype(BF16)
         owner_lines = lax.broadcasted_iota(jnp.int32, (plane, size), 0)
         rank_lines = lax.broadcasted_iota(jnp.int32, (cap, size), 0)
-        pieces, most = [], None
+        pieces = []
         for g in range(ny):
             owner = pairs_all[g, 0:1, :].astype(jnp.int32)
             row = pairs_all[g, 1:2, :]
@@ -205,21 +209,18 @@
                 (member * low).astype(BF16), at_rank, (1, 1)
             )
             pieces.append(jnp.where(found > 0.5, ids, float(ITEMS_DEV)))
-            count = jnp.sum(member, axis=1, keepdims=True)
-            most = count if most is None else jnp.maximum(most, count)
-        spare = ids_ref.shape[2] - ny * cap
-        pieces.append(jnp.broadcast_to(most, (plane, spare)))
+        spare = ids_out.shape[2] - ny * cap
+        pieces.append(jnp.zeros((plane, spare), F32))
         named = jnp.concatenate(pieces, axis=1).astype(jnp.int32)
         ids_out[...] = named.reshape(ids_out.shape)
 
     with jax.named_scope("users"):
-        for r in range(1, nx // 2 + 1):
-            x_forward(r)
-            if r == 1:
-                z_forward(1)
-                for step in range(1, ny):
-                    arrived(pairs_all.at[y_at(-step)], i_recv.at[step])
-                name_slots()
+        for r in (1, 2):
+            for parts in (early, late):
+                if r < nz // 2 or parts is early:
+                    z_forward(r, parts)
+                if r <= nx // 2:
+                    x_forward(r, parts)
         from_partner()
 
     def first_pass(chunk):
@@ -234,25 +235,46 @@
             peaks[chunk, k : k + 1, :] = top
             sums[chunk, k : k + 1, :] = jnp.sum(p, axis=0, keepdims=True)
 
+    batch, batches = peers, nz
+    high_span = acc.shape[1]
+    low_count = acc.shape[0] // share
+
+    def read_slots():
+        @pl.loop(1, plane)
+        def _(step):
+            arrived(ids_land.at[from_far(step)], n_recv.at[step])
+            arrived(ids_out.at[0], n_send.at[step])
+
+        rows = ids_land[...].reshape(plane, ids_land.shape[2]).astype(F32)
+        low = jnp.floor(rows * (1.0 / high_span))
+        high = rows - high_span * low
+        lanes = (ids_land.shape[2], batch * cap)
+        slot_of = lax.broadcasted_iota(jnp.int32, lanes, 0)
+        place_of = lax.rem(lax.broadcasted_iota(jnp.int32, lanes, 1), cap)
+        at = (plane, batch * cap)
+        mine = lax.rem(lax.broadcasted_iota(jnp.int32, at, 0), batch) == (
+            lax.broadcasted_iota(jnp.int32, at, 1) // cap
+        )
+        for g in range(ny):
+            spread = (slot_of == place_of + g * cap).astype(BF16)
+            for part, keep in ((low, low_all), (high, high_all)):
+                wide = jnp.dot(part.astype(BF16), spread, preferred_element_type=F32)
+                wide = jnp.where(mine, wide, 0.0).reshape(batches, batch, batch * cap)
+                keep[g] = jnp.sum(wide, axis=1).astype(jnp.int32)
+
     with jax.named_scope("first"):
         first_pass(z)
-
-        @pl.loop(1, plane)
-        def _(step):
-            where, there = far(step)
-            send_plainly(ids_out.at[there], ids_ref.at[here], n_send.at[step], n_recv.at[step], where)
-
-        ids_ref[here] = ids_out[here]
-        for r in range(1, nz // 2 + 1):
-            if r > 1:
-                z_forward(r)
-            if r < nz // 2:
-                @pl.loop(0, 2)
-                def _(side):
-                    first_pass(lax.rem(z + nz + r - 2 * r * side, nz))
-            else:
-                first_pass(z_at(r))
-
+        for r in range(1, nz // 2):
+            if 2 < r + 1 < nz // 2:
+                z_forward(r + 1, early)
+
+            @pl.loop(0, 2)
+            def _(side):
+                first_pass(lax.rem(z + nz + r - 2 * r * side, nz))
+
+            if 2 < r + 1:
+                z_forward(r + 1, late if r + 1 < nz // 2 else early)
+        first_pass(z_at(nz // 2))
     with jax.named_scope("lse"):
         tops = peaks[...]
         top = jnp.max(tops, axis=0)
@@ -314,53 +336,72 @@
     def user_pass(k):
         gu_part[k] = jnp.dot(items_turned[...], ds[:, block_rows(k)], preferred_element_type=F32)
 
+    def collected(own, land, n):
+        pieces = []
+        for half in (0, 1):
+            got = own[half * half_size : (half + 1) * half_size]
+            for way in (0, 1):
+                length = chain_length(n, way, half)
+                if length:
+                    got = got + land[way, half, length - 1]
+            pieces.append(got)
+        return jnp.concatenate(pieces, axis=0)
+
+
+    def x_reduce(r, parts_of):
+        for way, half in parts_of:
+            sign = signs[way]
+            length = chain_length(nx, way, half)
+            rows = pl.ds(half * half_size, half_size)
+            dest = x_at(sign * (length - r))
+            if 1 <= r <= length:
+                land = x_land.at[way, half, r - 1]
+                arrived(land, xr_recv.at[way, half, r - 1])
+                if r < length:
+                    land[...] += gu_pair[dest, rows]
+            if r < length:
+                src = gu_pair.at[dest, rows] if r == 0 else x_land.at[way, half, r - 1]
+                send(src, x_land.at[way, half, r], xr_send.at[way, half, r],
+                     xr_recv.at[way, half, r], {"rows_1": x_at(sign)})
+
     with jax.named_scope("zr1"):
-        z_reduce(1)
+        z_reduce(1, early)
     with jax.named_scope("userpass"):
         for step in range(nx):
             k = x_at(step) * nc + 1 - c
             user_pass(k)
             send(gu_part.at[k], gu_pair.at[x_at(step)], d_send.at[step], d_recv.at[step], partner)
-        for step in range(nx):
+        for step in range(nx // 2):
+            user_pass(x_at(step) * nc + c)
+        z_reduce(1, late)
+        for step in range(nx // 2, nx):
             user_pass(x_at(step) * nc + c)
         for step in range(nx):
             arrived(gu_pair.at[x_at(step)], d_recv.at[step])
             gu_pair[x_at(step)] += gu_part[x_at(step) * nc + c]
-
-    def x_reduce(r):
-        for way, sign in enumerate(signs):
-            for half in (0, 1):
-                length = chain_length(nx, way, half)
-                rows = pl.ds(half * half_size, half_size)
-                dest = x_at(sign * (length - r))
-                if 1 <= r <= length:
-                    land = x_land.at[way, half, r - 1]
-                    arrived(land, xr_recv.at[way, half, r - 1])
-                    if r < length:
-                        land[...] += gu_pair[dest, rows]
-                if r < length:
-                    src = gu_pair.at[dest, rows] if r == 0 else x_land.at[way, half, r - 1]
-                    send(src, x_land.at[way, half, r], xr_send.at[way, half, r],
-                         xr_recv.at[way, half, r], {"rows_1": x_at(sign)})
-
     with jax.named_scope("reduce"):
-        x_reduce(0)
-        for r in range(1, nx // 2 + 1):
-            if r + 1 <= nz // 2:
-                z_reduce(r + 1)
-            x_reduce(r)
-
-        def collected(own, land, n):
-            pieces = []
-            for half in (0, 1):
-                got = own[half * half_size : (half + 1) * half_size]
-                for way in (0, 1):
-                    length = chain_length(n, way, half)
-                    if length:
-                        got = got + land[way, half, length - 1]
-                pieces.append(got)
-            return jnp.concatenate(pieces, axis=0)
-
+        x_reduce(0, early)
+        x_reduce(0, late)
+        for step in range(1, ny):
+            arrived(pairs_all.at[y_at(-step)], i_recv.at[step])
+        name_slots()
+
+        @pl.loop(1, plane)
+        def _(step):
+            where, there = far(step)
+            send_plainly(ids_out.at[there], ids_land.at[here], n_send.at[step], n_recv.at[step], where)
+
+        ids_land[here] = ids_out[here]
+        along_z = [(r, parts) for r in range(2, nz // 2) for parts in (early, late)]
+        along_x = [(r, parts) for r in range(1, nx // 2 + 1) for parts in (early, late)]
+        for event in along_z[:2]:
+            z_reduce(*event)
+        along_z = along_z[2:]
+        while along_z or along_x:
+            if along_x:
+                x_reduce(*along_x.pop(0))
+            if along_z:
+                z_reduce(*along_z.pop(0))
     with jax.named_scope("towerback"):
         gu = collected(gu_pair[x], x_land, nx).astype(BF16)
         pre = pre_keep[...]
@@ -372,8 +413,7 @@
 
     with jax.named_scope("zrlast"):
         send(df_keep.at[1 - c], df_pair, ac_send, ac_recv, partner)
-        for r in range(nx // 2 + 2, nz // 2 + 1):
-            z_reduce(r)
+        z_reduce(nz // 2, early)
         gi = collected(gi_part[z], z_land, nz).astype(BF16)
     with jax.named_scope("shares"):
         for to in range(ny):
@@ -389,6 +429,8 @@
         for step in range(1, ny):
             send(y_part.at[y_at(step)], y_land.at[step - 1], ay_send.at[step], ay_recv.at[step],
                  {"grp": y_at(step)})
+    with jax.named_scope("readslots"):
+        read_slots()
     with jax.named_scope("sharewait"):
         for step in range(1, ny):
             arrived(share_in.at[y_at(-step)], s_recv.at[step])
@@ -406,13 +448,16 @@
 
         def exchange(first, last):
             @pl.loop(first, last)
-            def _(step):
+            def _(turn):
+                pick, odd = turn // peers // 2, lax.rem(turn // peers, 2)
+                dz = (1 - odd) * (nz // 2 + pick) + odd * (nz // 2 - 1 - pick)
+                step = dz * peers + peers - 1 - lax.rem(turn, peers)
                 where, there = far(step)
-                send_plainly(slotted.at[there], got_ref.at[here], e_send.at[step], e_recv.at[step],
+                send_plainly(slotted.at[there], landed.at[here], e_send.at[step], e_recv.at[step],
                              where)
 
-        exchange(1, plane // 4)
-        got_ref[here] = slotted[here]
+        landed[here] = slotted[here]
+        acc[...] = jnp.zeros_like(acc)
     with jax.named_scope("ysum"):
         whole = y_part[y]
         for step in range(1, ny):
@@ -425,14 +470,15 @@
             where, there = far_tile(step)
             send_plainly(p_part.at[there], p_land.at[step], ap_send.at[step], ap_recv.at[step], where)
 
-        exchange(plane // 4, plane // 2)
+        exchange(0, plane // 4)
         p_land[0] = p_part[tile]
     with jax.named_scope("planesum"):
         @pl.loop(1, tiles)
         def _(step):
             arrived(p_land.at[step], ap_recv.at[step])
-
-        own = tower_ref.at[c, y, tile]
+            arrived(p_part.at[0], ap_send.at[step])
+
+        own = tower.at[c, y, tile]
         own[...] = jnp.sum(p_land[...], axis=0)
 
         @pl.loop(1, tiles)
@@ -440,42 +486,64 @@
             where, _ = far_tile(step)
             send_plainly(own, own, gp_send.at[step], gp_recv.at[step], where)
 
-        exchange(plane // 2, plane)
+        exchange(plane // 4, plane - 1)
+    long = batch * cap
+
+    def add_rows(b):
+        for unit, dz in enumerate((nz // 2 + b, nz // 2 - 1 - b)):
+            @pl.loop(0 if dz else 1, peers)
+            def _(inner):
+                arrived(landed.at[from_far(dz * peers + inner)], e_recv.at[dz * peers + inner])
+                arrived(slotted.at[0], e_send.at[dz * peers + inner])
+
+            source = z_at(-dz)
+            for pair in range(ny // 2):
+                block = landed[pl.ds(source * batch, batch), pair].reshape(long, 2 * share)
+                turned = block.T
+                for side in (0, 1):
+                    g = 2 * pair + side
+                    data = turned[side * share : (side + 1) * share, :]
+                    low = low_all[g, pl.ds(source, 1), :]
+                    cols = slice((2 * g + unit) * long, (2 * g + unit + 1) * long)
+                    for at in range(low_count):
+                        spread_left[at * share : (at + 1) * share, cols] = data * (
+                            low == at
+                        ).astype(BF16)
+                    lines_of = lax.broadcasted_iota(jnp.int32, (high_span, long), 0)
+                    high = high_all[g, pl.ds(source, 1), :]
+                    spread_right[:, cols] = (lines_of == high).astype(BF16)
+        acc[...] += contract(spread_left[...], spread_right[...], (1, 1))
+
+    with jax.named_scope("add0"):
+        add_rows(0)
     with jax.named_scope("planeback"):
-
         @pl.loop(1, tiles)
         def _(step):
-            arrived(tower_ref.at[c, y, from_far_tile(step)], gp_recv.at[step])
-
+            arrived(tower.at[c, y, from_far_tile(step)], gp_recv.at[step])
+            arrived(p_part.at[0], gp_send.at[step])
+
+        for step in range(1, ny):
+            send(tower.at[c, y], tower.at[c, y], gy_send.at[step], gy_recv.at[step],
+                 {"grp": y_at(step)})
+    with jax.named_scope("add1"):
+        for b in range(1, nz // 2 - 1):
+            add_rows(b)
     with jax.named_scope("yback"):
         for step in range(1, ny):
-            send(tower_ref.at[c, y], tower_ref.at[c, y], gy_send.at[step], gy_recv.at[step],
-                 {"grp": y_at(step)})
-        for step in range(1, ny):
-            arrived(tower_ref.at[c, y_at(-step)], gy_recv.at[step])
-        send(tower_ref.at[c], tower_ref.at[c], gc_send, gc_recv, partner)
-
-    with jax.named_scope("got"):
-        @pl.loop(1, plane)
-        def _(step):
-            arrived(ids_ref.at[from_far(step)], n_recv.at[step])
-            arrived(got_ref.at[from_far(step)], e_recv.at[step])
-
+            arrived(tower.at[c, y_at(-step)], gy_recv.at[step])
+        send(tower.at[c], tower.at[c], gc_send, gc_recv, partner)
+    with jax.named_scope("add3"):
+        add_rows(nz // 2 - 1)
+        for at in range(low_count):
+            table_ref[:, at * high_span : (at + 1) * high_span] = acc[at * share : (at + 1) * share, :]
     with jax.named_scope("cback"):
-        arrived(tower_ref.at[1 - c], gc_recv)
+        arrived(tower.at[1 - c], gc_recv)
+        width = first_ref.shape[0]
+        first_ref[...] = tower[0].reshape(width, width).T
+        second_ref[...] = tower[1].reshape(width, width).T
     with jax.named_scope("sent"):
         for copy in pending:
             copy.wait_send()
-
-        @pl.loop(1, plane)
-        def _(step):
-            arrived(ids_out.at[0], n_send.at[step])
-            arrived(slotted.at[0], e_send.at[step])
-
-        @pl.loop(1, tiles)
-        def _(step):
-            arrived(p_part.at[0], ap_send.at[step])
-            arrived(p_part.at[0], gp_send.at[step])
 
 
 def block_grads(features, w_first, w_second, items, *columns):
@@ -493,9 +561,9 @@
     return pl.pallas_call(
         functools.partial(block_kernel, nz, nx, nc, ny),
         out_shape=(
-            jax.ShapeDtypeStruct((plane, ny // 2, cap, 2 * share), BF16),
-            jax.ShapeDtypeStruct((plane, 1, lane), jnp.int32),
-            jax.ShapeDtypeStruct(tower, F32),
+            jax.ShapeDtypeStruct((share, ITEMS_DEV), F32),
+            jax.ShapeDtypeStruct((width, width), F32),
+            jax.ShapeDtypeStruct((width, width), F32),
         ),
         in_specs=[pl.BlockSpec(memory_space=vmem)] * 8,
         out_specs=[pl.BlockSpec(memory_space=vmem)] * 3,
@@ -547,6 +615,14 @@
             dma((tiles,)), dma((tiles,)),
             dma((ny,)), dma((ny,)),
             dma, dma,
+            vmem((plane, ny // 2, cap, 2 * share), BF16),
+            vmem((plane, 1, lane), jnp.int32),
+            vmem(tower, F32),
+            vmem((ny, nz, peers * cap), jnp.int32),
+            vmem((ny, nz, peers * cap), jnp.int32),
+            vmem((ITEMS_DEV // HIGH * share, ny * 2 * peers * cap), BF16),
+            vmem((HIGH, ny * 2 * peers * cap), BF16),
+            vmem((ITEMS_DEV // HIGH * share, HIGH), F32),
         ],
         compiler_params=pltpu.CompilerParams(
             collective_id=0, has_side_effects=True, vmem_limit_bytes=60 * 2**20
@@ -556,67 +632,36 @@
     )(features, w_first, w_second, items, *columns)
 
 
-def table_kernel(ids_ref, got_ref, tower_ref, out_ref, first_ref, second_ref, lines, *tables):
-    sources, pairs, cap, lanes = got_ref.shape
-    share = lanes // 2
-    width = first_ref.shape[0]
-    count = out_ref.shape[1]
-    step = 4
-    lines[...] = got_ref[...].astype(F32).reshape(lines.shape)
-    for table in tables:
-        table[...] = jnp.zeros_like(table)
-
-    @pl.loop(0, sources)
-    def _(source):
-        @pl.loop(0, (ids_ref[source, 2 * pairs * cap] + (step - 1)) // step)
-        def _(block):
-            for slot in range(step):
-                slot = block * step + slot
-                for pair in range(pairs):
-                    line = lines[pl.ds((source * pairs + pair) * cap + slot, 1), :]
-                    for side in (0, 1):
-                        g = 2 * pair + side
-                        at = pl.ds(ids_ref[source, g * cap + slot], 1)
-                        tables[g][at, :] += line
-
-    part = min(count, 512)
-    for at in range(0, count, part):
-        rows = slice(at, at + part)
-        even = sum(t[rows, :] for t in tables[0::2])
-        odd = sum(t[rows, :] for t in tables[1::2])
-        out_ref[:, rows] = even.T[:share, :] + odd.T[share:, :]
-    first_ref[...] = tower_ref[0].reshape(width, width).T
-    second_ref[...] = tower_ref[1].reshape(width, width).T
-
-
-def table_grads(ids, got, tower):
-    sources, pairs, cap, lanes = got.shape
-    width = tower.shape[-1]
-    vmem = pltpu.VMEM
+def finish_kernel(*refs):
+    count = (len(refs) - 1) // 2
+    copies = [
+        pltpu.make_async_copy(refs[i], refs[count + i], refs[-1].at[i]) for i in range(count)
+    ]
+    for copy in copies:
+        copy.start()
+    for copy in copies:
+        copy.wait()
+
+
+def finish(*arrays):
     return pl.pallas_call(
-        table_kernel,
-        out_shape=(
-            jax.ShapeDtypeStruct((lanes // 2, ITEMS_DEV), F32),
-            jax.ShapeDtypeStruct((width, width), F32),
-            jax.ShapeDtypeStruct((width, width), F32),
-        ),
-        in_specs=[pl.BlockSpec(memory_space=pltpu.SMEM)] + [pl.BlockSpec(memory_space=vmem)] * 2,
-        out_specs=[pl.BlockSpec(memory_space=vmem)] * 3,
-        scratch_shapes=[vmem((sources * pairs * cap, lanes), F32)]
-        + [vmem((ITEMS_DEV + 8, lanes), F32)] * (2 * pairs),
-        compiler_params=pltpu.CompilerParams(vmem_limit_bytes=40 * 2**20),
-        name="table_grads",
-    )(ids, got, tower)
+        finish_kernel,
+        out_shape=tuple(jax.ShapeDtypeStruct(a.shape, a.dtype) for a in arrays),
+        in_specs=[pl.BlockSpec(memory_space=pl.ANY)] * len(arrays),
+        out_specs=[pl.BlockSpec(memory_space=pltpu.VMEM)] * len(arrays),
+        scratch_shapes=[pltpu.SemaphoreType.DMA((len(arrays),))],
+        name="finish",
+    )(*arrays)
 
 
 def body(
     user_features, w_first, w_second, item_embed, example_weight, positive, item_owner, item_row
 ):
-    got, ids, tower = block_grads(
+    table, first, second = block_grads(
         user_features[0], w_first, w_second, item_embed[0],
         example_weight, positive, item_owner.reshape(positive.shape), item_row,
     )
-    table, first, second = table_grads(ids.reshape(ids.shape[0], -1), got, tower)
+    table, first, second = finish(table, first, second)
     return (first, second, table.T)
 
 

time: 122 us -> 98.4 us (0.81); the launches traced: 124 us -> 98.3 us
  Pallas kernels: 120 us -> 97.5 us
  local copies, waits for them, and re-layouts: 2.83 us -> 0 us
    pallas_call x1, Pallas kernels: 15.4 us -> 2.5 us  [finish(): pl.pallas_call(finish_kernel, out_shape=tuple((jax.ShapeDtypeStruct(a.sha...]
    pallas_call x1, Pallas kernels: 105 us -> 95 us  [block_grads(): pl.pallas_call(functools.partial(block_kernel, nz, nx, nc, ny), out_shape...]
    unnamed x6 -> x0, local copies, waits for them, and re-layouts: 2.83 us -> none
where the time goes in v4:
time: 98.4 us; the launch traced here: 98.3 us
  Pallas kernels  97.5 us (99%)
    pallas_call x1, Pallas kernels, block_grads(): pl.pallas_call(functools.partial(block_kernel, nz, nx, nc, ny), out_shape...  95 us
    pallas_call x1, Pallas kernels, finish(): pl.pallas_call(finish_kernel, out_shape=tuple((jax.ShapeDtypeStruct(a.sha...  2.5 us

profile of v4, /device:TPU:1, one launch (start us, length us, event | category | flops | bytes accessed | tf_op | source)
XLA Modules:
  0.0 98.3 jit_solution(17472032873480082459)
XLA Ops:
  0.6 95.0 %block_grads.1 = (f32[64,4096]{1,0:T(8,128)}, f32[256,256]{1,0:T(8,128)}, f32[256,256]{1,0:T(8,128)}) custom-call(bf16[256,256]{1,0:T(8,128)(2,1)} %bitcast.5, bf16[256,256]{1,0:T(8,128)(2,1)} %w1_ref.1, bf16[256,256]{1,0:T(8,128)(2,1)} %w2_ref.1, bf16[256,256]{1,0:T(8,128)(2,1)} %bitcast.6, f32[1,256]{1,0:T(1,128)} %weight_ref.1, s32[1,256]{1,0:T(1,128)} %target_ref.1, ...), custom_call_target="tpu_custom_call" | custom-call | flops 7000000000 | bytes 1048576 | tf_op jit(solution)/shard_map/block_grads/pallas_call | solution.py:561
  95.6 2.5 %finish.1 = (f32[64,4096]{1,0:T(8,128)}, f32[256,256]{1,0:T(8,128)}, f32[256,256]{1,0:T(8,128)}) custom-call(f32[64,4096]{1,0:T(8,128)} %get-tuple-element.9.refs_0_, f32[256,256]{1,0:T(8,128)} %get-tuple-element.10.refs_1_, f32[256,256]{1,0:T(8,128)} %get-tuple-element.11.refs_2_), custom_call_target="tpu_custom_call" | custom-call | tf_op jit(solution)/shard_map/finish/pallas_call | solution.py:647

commit v5 on v4

--- a/solution.py
+++ b/solution.py
@@ -446,12 +446,13 @@
             both = jnp.concatenate(sides, axis=1).astype(BF16)
             slotted[:, pair] = both.reshape(plane, cap, 2 * share)
 
-        def exchange(first, last):
-            @pl.loop(first, last)
-            def _(turn):
-                pick, odd = turn // peers // 2, lax.rem(turn // peers, 2)
-                dz = (1 - odd) * (nz // 2 + pick) + odd * (nz // 2 - 1 - pick)
-                step = dz * peers + peers - 1 - lax.rem(turn, peers)
+        turns = {8: (4, 5, 6, 3, 7, 2, 1, 0), 4: (2, 3, 1, 0)}[nz]
+        ahead = nz // 2 - 1
+
+        def exchange(dz):
+            @pl.loop(0 if dz else 1, peers)
+            def _(inner):
+                step = dz * peers + inner
                 where, there = far(step)
                 send_plainly(slotted.at[there], landed.at[here], e_send.at[step], e_recv.at[step],
                              where)
@@ -470,9 +471,19 @@
             where, there = far_tile(step)
             send_plainly(p_part.at[there], p_land.at[step], ap_send.at[step], ap_recv.at[step], where)
 
-        exchange(0, plane // 4)
+        for dz in turns[:ahead]:
+            exchange(dz)
         p_land[0] = p_part[tile]
     with jax.named_scope("planesum"):
+        long = batch * cap
+        lines_of = lax.broadcasted_iota(jnp.int32, (high_span, long), 0)
+        for b in range(nz // 2):
+            for unit, dz in enumerate(turns[2 * b : 2 * b + 2]):
+                for g in range(ny):
+                    high = high_all[g, pl.ds(z_at(-dz), 1), :]
+                    cols = slice((2 * g + unit) * long, (2 * g + unit + 1) * long)
+                    spread_right[b, :, cols] = (lines_of == high).astype(BF16)
+
         @pl.loop(1, tiles)
         def _(step):
             arrived(p_land.at[step], ap_recv.at[step])
@@ -486,11 +497,10 @@
             where, _ = far_tile(step)
             send_plainly(own, own, gp_send.at[step], gp_recv.at[step], where)
 
-        exchange(plane // 4, plane - 1)
-    long = batch * cap
-
+        for dz in turns[ahead:]:
+            exchange(dz)
     def add_rows(b):
-        for unit, dz in enumerate((nz // 2 + b, nz // 2 - 1 - b)):
+        for unit, dz in enumerate(turns[2 * b : 2 * b + 2]):
             @pl.loop(0 if dz else 1, peers)
             def _(inner):
                 arrived(landed.at[from_far(dz * peers + inner)], e_recv.at[dz * peers + inner])
@@ -509,10 +519,7 @@
                         spread_left[at * share : (at + 1) * share, cols] = data * (
                             low == at
                         ).astype(BF16)
-                    lines_of = lax.broadcasted_iota(jnp.int32, (high_span, long), 0)
-                    high = high_all[g, pl.ds(source, 1), :]
-                    spread_right[:, cols] = (lines_of == high).astype(BF16)
-        acc[...] += contract(spread_left[...], spread_right[...], (1, 1))
+        acc[...] += contract(spread_left[...], spread_right[b], (1, 1))
 
     with jax.named_scope("add0"):
         add_rows(0)
@@ -621,7 +628,7 @@
             vmem((ny, nz, peers * cap), jnp.int32),
             vmem((ny, nz, peers * cap), jnp.int32),
             vmem((ITEMS_DEV // HIGH * share, ny * 2 * peers * cap), BF16),
-            vmem((HIGH, ny * 2 * peers * cap), BF16),
+            vmem((nz // 2, HIGH, ny * 2 * peers * cap), BF16),
             vmem((ITEMS_DEV // HIGH * share, HIGH), F32),
         ],
         compiler_params=pltpu.CompilerParams(

time: 98.4 us -> 97.6 us (level)
  no operation moved by 1% of the time
where the time goes in v5:
time: 97.6 us; the launch traced here: 97.4 us
  Pallas kernels  96.6 us (99%)
    pallas_call x1, Pallas kernels, block_grads(): pl.pallas_call(functools.partial(block_kernel, nz, nx, nc, ny), out_shape...  94.1 us
    pallas_call x1, Pallas kernels, finish(): pl.pallas_call(finish_kernel, out_shape=tuple((jax.ShapeDtypeStruct(a.sha...  2.5 us

profile of v5, /device:TPU:1, one launch (start us, length us, event | category | flops | bytes accessed | tf_op | source)
XLA Modules:
  0.0 97.4 jit_solution(17816310156928761078)
XLA Ops:
  0.6 94.1 %block_grads.1 = (f32[64,4096]{1,0:T(8,128)}, f32[256,256]{1,0:T(8,128)}, f32[256,256]{1,0:T(8,128)}) custom-call(bf16[256,256]{1,0:T(8,128)(2,1)} %bitcast.5, bf16[256,256]{1,0:T(8,128)(2,1)} %w1_ref.1, bf16[256,256]{1,0:T(8,128)(2,1)} %w2_ref.1, bf16[256,256]{1,0:T(8,128)(2,1)} %bitcast.6, f32[1,256]{1,0:T(1,128)} %weight_ref.1, s32[1,256]{1,0:T(1,128)} %target_ref.1, ...), custom_call_target="tpu_custom_call" | custom-call | flops 7000000000 | bytes 1048576 | tf_op jit(solution)/shard_map/block_grads/pallas_call | solution.py:568
  94.8 2.5 %finish.1 = (f32[64,4096]{1,0:T(8,128)}, f32[256,256]{1,0:T(8,128)}, f32[256,256]{1,0:T(8,128)}) custom-call(f32[64,4096]{1,0:T(8,128)} %get-tuple-element.9.refs_0_, f32[256,256]{1,0:T(8,128)} %get-tuple-element.10.refs_1_, f32[256,256]{1,0:T(8,128)} %get-tuple-element.11.refs_2_), custom_call_target="tpu_custom_call" | custom-call | tf_op jit(solution)/shard_map/finish/pallas_call | solution.py:654
